TPU v7x, 8 devices: a whole 2x2x1 slice. The times are simulated.
8 devices in a mesh: model: 1 (over z), replica: 2 (over y), fsdp: 4 (over x, core).
Axes of the slice: x: 2, y: 2, z: 1, core: 2. Of those that a mesh axis runs over, the one named last changes fastest.
Arguments:
- x_in: bfloat16 [3, 8192, 2048], P(None, ('model', 'replica', 'fsdp'))
- dy_out: bfloat16 [3, 8192, 2048], P(None, ('model', 'replica', 'fsdp'))
- lengths: int32 [3, 8], P(None, ('model', 'replica', 'fsdp'))
- w_up: bfloat16 [1, 2048, 8192], P(None, ('model', 'fsdp'))
- w_down: bfloat16 [1, 8192, 2048], P(None, ('model', 'fsdp'))
Outputs:
- output 1: float32 [1, 2048, 8192], P(None, ('model', 'fsdp'))
- output 2: float32 [1, 8192, 2048], P(None, ('model', 'fsdp'))
All inputs are finite; a program needn't handle non-finite values.
Results may differ from a plain program's by a relative error of at most 0.001.
Values are sent between devices in bfloat16 or wider.
A program may use at most 1 GiB of HBM per device.

v0:
```python
import jax
import jax.numpy as jnp
from jax import lax
from jax.sharding import PartitionSpec as P, NamedSharding


def gather_full(w_shard):
    return lax.all_gather(w_shard, "fsdp", axis=0, tiled=True)


def solution(mesh):
    tok_spec = P(None, ("model", "replica", "fsdp"), None)
    len_spec = P(None, ("model", "replica", "fsdp"))
    w_spec = P(None, ("model", "fsdp"), None)

    def device_grads(x_in, dy_out, lengths, w_up, w_down):
        tok_dev = x_in.shape[1]
        n_layers = w_up.shape[0]
        token_mask = jnp.arange(tok_dev)[None, :] < lengths

        def micro_step(acc_pair, micro_in):
            x_cur, dy_cur, mask_cur = micro_in
            saved_acts = []
            for layer_idx in range(n_layers):
                up_full = gather_full(w_up[layer_idx])
                hidden = jnp.dot(x_cur, up_full, preferred_element_type=jnp.float32).astype(jnp.bfloat16)
                saved_acts.append((x_cur, hidden))
                if layer_idx + 1 < n_layers:
                    down_full = gather_full(w_down[layer_idx])
                    act_bf = jax.nn.gelu(hidden.astype(jnp.float32)).astype(jnp.bfloat16)
                    x_cur = (x_cur.astype(jnp.float32) + jnp.dot(act_bf, down_full, preferred_element_type=jnp.float32)).astype(jnp.bfloat16)
            grad_x = jnp.where(mask_cur[:, None], dy_cur, jnp.zeros_like(dy_cur))
            new_up = list(acc_pair[0])
            new_down = list(acc_pair[1])
            for layer_idx in reversed(range(n_layers)):
                x_prev, hidden = saved_acts[layer_idx]
                down_full = gather_full(w_down[layer_idx])
                act_f32, gelu_vjp = jax.vjp(jax.nn.gelu, hidden.astype(jnp.float32))
                act_bf = act_f32.astype(jnp.bfloat16)
                grad_act = jnp.einsum("td,fd->tf", grad_x, down_full, preferred_element_type=jnp.float32)
                grad_hid = gelu_vjp(grad_act)[0].astype(jnp.bfloat16)
                gw_down = jnp.einsum("tf,td->fd", act_bf, grad_x, preferred_element_type=jnp.float32)
                gw_up = jnp.einsum("td,tf->df", x_prev, grad_hid, preferred_element_type=jnp.float32)
                if layer_idx > 0:
                    up_full = gather_full(w_up[layer_idx])
                    grad_x = (grad_x.astype(jnp.float32) + jnp.einsum("tf,df->td", grad_hid, up_full, preferred_element_type=jnp.float32)).astype(jnp.bfloat16)
                new_up[layer_idx] = new_up[layer_idx] + lax.psum_scatter(gw_up, "fsdp", scatter_dimension=0, tiled=True)
                new_down[layer_idx] = new_down[layer_idx] + lax.psum_scatter(gw_down, "fsdp", scatter_dimension=0, tiled=True)
            return (tuple(new_up), tuple(new_down)), None

        init_up = tuple(jnp.zeros(w_up.shape[1:], jnp.float32) for layer_idx in range(n_layers))
        init_down = tuple(jnp.zeros(w_down.shape[1:], jnp.float32) for layer_idx in range(n_layers))
        (acc_up, acc_down), _ = lax.scan(micro_step, (init_up, init_down), (x_in, dy_out, token_mask))
        grad_up = lax.psum(jnp.stack(acc_up), "replica")
        grad_down = lax.psum(jnp.stack(acc_down), "replica")
        return grad_up, grad_down

    return jax.shard_map(device_grads, mesh=mesh, in_specs=(tok_spec, tok_spec, len_spec, w_spec, w_spec), out_specs=(w_spec, w_spec), check_vma=False)
```

profile of v0, /device:TPU:0, one launch (start us, length us, event | category | flops | bytes accessed | tf_op | source)
XLA Modules:
  0.0 5007.9 jit_solution(3301851003596373294)
XLA Ops:
  8.0 0.7 iota_compare_fusion
  8.7 4233.4 %while.15 = (s32[]{:T(128)}, f32[512,8192]{1,0:T(8,128)}, f32[2048,2048]{1,0:T(8,128)}, bf16[3,1024,2048]{2,1,0:T(8,128)(2,1)}, pred[3,1024]{1,0:T(4,128)(4,1)S(...) while((s32[]{:T(128)}, f32[512,8192]{1,0:T(8,128)}, ...), condition=%wide.region_3.4_spmd.clone, body=%wide.region_0.3_spmd.clone.sunk | while | flops 137728360448 | bytes 1157658880 | solution.py:53
  8.8 0.7 all-gather.11.cloned.1.call-update
  9.5 0.7 all-gather.13.cloned.1.call-update
  10.2 0.0 reduce-scatter.11.cloned.1.call-start
  10.3 203.0 %all-gather.11.cloned.1.call-done = bf16[1,2048,8192]{2,1,0:T(8,128)(2,1)} async-done(((bf16[1,512,8192]{2,1,0:T(8,128)(2,1)}), bf16[1,2048,8192]{2,1,0:T(8,128)(2,1)}) %all-gather.11.cloned.1.call-update) | async-done | bytes 33554448 | tf_op jit(solution)/shard_map/while/body/eval_jaxpr/all_gather | solution.py:8
  213.3 41.8 fusion.78
  255.1 159.1 %all-gather.13.cloned.1.call-done = bf16[1,8192,2048]{2,1,0:T(8,128)(2,1)} async-done(((bf16[1,2048,2048]{2,1,0:T(8,128)(2,1)}), bf16[1,8192,2048]{2,1,0:T(8,128)(2,1)}) %all-gather.13.cloned.1.call-update) | async-done | bytes 33554448 | tf_op jit(solution)/shard_map/while/body/eval_jaxpr/all_gather | solution.py:8
  414.2 62.7 %fusion.79 = bf16[1024,8192]{1,0:T(8,128)(2,1)} fusion(bf16[1024,8192]{1,0:T(8,128)(2,1)} %fusion.78, bf16[1,8192,2048]{2,1,0:T(8,128)(2,1)} %all-gather.13.cloned.1.call-done, bf16[3,1024,2048]{2,1,0:T(8,128)(2,1)} %get-tuple-element.225, s32[]{:T(128)} %get-tuple-element.210, pred[1024]{0:T(1024)(128)(4,1)S(1)} %dynamic-slice_reduce_fusion.2), kind=kOutput, calls=%fused_computation.8.clone.clone.2.clone.1 | convolution fusion | flops 34537996288 | bytes 71304704 | tf_op jit(solution)/shard_map/while/body/eval_jaxpr/td,fd->tf/dot_general | solution.py:40
  476.9 45.2 fusion.80
  522.1 0.0 reduce-scatter.13.cloned.1.call-start
  522.1 52.9 %fusion.81 = f32[8192,2048]{1,0:T(8,128)} fusion(bf16[1024,8192]{1,0:T(8,128)(2,1)} %fusion.78, bf16[3,1024,2048]{2,1,0:T(8,128)(2,1)} %get-tuple-element.225, s32[]{:T(128)} %get-tuple-element.210, pred[1024]{0:T(1024)(128)(4,1)S(1)} %dynamic-slice_reduce_fusion.2), kind=kOutput, calls=%fused_computation.19.clone.1 | convolution fusion | flops 34445721600 | bytes 88081920 | tf_op jit(solution)/shard_map/while/body/eval_jaxpr/tf,td->fd/dot_general | solution.py:42
  575.1 387.8 %reduce-scatter.11.cloned.1.call-done = f32[512,8192]{1,0:T(8,128)} async-done(((f32[2048,8192]{1,0:T(8,128)}), f32[512,8192]{1,0:T(8,128)}) %reduce-scatter.11.cloned.1.call-update) | async-done | bytes 16777232 | tf_op jit(solution)/shard_map/while
  962.8 11.9 select_add_fusion.4
  974.7 431.2 %reduce-scatter.13.cloned.1.call-done = f32[2048,2048]{1,0:T(8,128)} async-done(((f32[8192,2048]{1,0:T(8,128)}), f32[2048,2048]{1,0:T(8,128)}) %reduce-scatter.13.cloned.1.call-update) | async-done | bytes 16777232 | tf_op jit(solution)/shard_map/while
  1405.8 13.1 select_add_fusion.5
  1419.0 0.5 all-gather.11.cloned.1.call-update
  1419.5 0.5 all-gather.13.cloned.1.call-update
  1420.2 200.2 %all-gather.11.cloned.1.call-done = bf16[1,2048,8192]{2,1,0:T(8,128)(2,1)} async-done(((bf16[1,512,8192]{2,1,0:T(8,128)(2,1)}), bf16[1,2048,8192]{2,1,0:T(8,128)(2,1)}) %all-gather.11.cloned.1.call-update) | async-done | bytes 33554448 | tf_op jit(solution)/shard_map/while/body/eval_jaxpr/all_gather | solution.py:8
  1620.3 41.8 fusion.78
  1662.1 159.0 %all-gather.13.cloned.1.call-done = bf16[1,8192,2048]{2,1,0:T(8,128)(2,1)} async-done(((bf16[1,2048,2048]{2,1,0:T(8,128)(2,1)}), bf16[1,8192,2048]{2,1,0:T(8,128)(2,1)}) %all-gather.13.cloned.1.call-update) | async-done | bytes 33554448 | tf_op jit(solution)/shard_map/while/body/eval_jaxpr/all_gather | solution.py:8
  1821.1 62.7 %fusion.79 = bf16[1024,8192]{1,0:T(8,128)(2,1)} fusion(bf16[1024,8192]{1,0:T(8,128)(2,1)} %fusion.78, bf16[1,8192,2048]{2,1,0:T(8,128)(2,1)} %all-gather.13.cloned.1.call-done, bf16[3,1024,2048]{2,1,0:T(8,128)(2,1)} %get-tuple-element.225, s32[]{:T(128)} %get-tuple-element.210, pred[1024]{0:T(1024)(128)(4,1)S(1)} %dynamic-slice_reduce_fusion.2), kind=kOutput, calls=%fused_computation.8.clone.clone.2.clone.1 | convolution fusion | flops 34537996288 | bytes 71304704 | tf_op jit(solution)/shard_map/while/body/eval_jaxpr/td,fd->tf/dot_general | solution.py:40
  1883.8 45.2 fusion.80
  1929.0 0.0 reduce-scatter.13.cloned.1.call-start
  1929.1 52.9 %fusion.81 = f32[8192,2048]{1,0:T(8,128)} fusion(bf16[1024,8192]{1,0:T(8,128)(2,1)} %fusion.78, bf16[3,1024,2048]{2,1,0:T(8,128)(2,1)} %get-tuple-element.225, s32[]{:T(128)} %get-tuple-element.210, pred[1024]{0:T(1024)(128)(4,1)S(1)} %dynamic-slice_reduce_fusion.2), kind=kOutput, calls=%fused_computation.19.clone.1 | convolution fusion | flops 34445721600 | bytes 88081920 | tf_op jit(solution)/shard_map/while/body/eval_jaxpr/tf,td->fd/dot_general | solution.py:42
  1982.0 387.7 %reduce-scatter.11.cloned.1.call-done = f32[512,8192]{1,0:T(8,128)} async-done(((f32[2048,8192]{1,0:T(8,128)}), f32[512,8192]{1,0:T(8,128)}) %reduce-scatter.11.cloned.1.call-update) | async-done | bytes 16777232 | tf_op jit(solution)/shard_map/while
  2369.7 17.9 select_add_fusion.4
  2387.6 425.2 %reduce-scatter.13.cloned.1.call-done = f32[2048,2048]{1,0:T(8,128)} async-done(((f32[8192,2048]{1,0:T(8,128)}), f32[2048,2048]{1,0:T(8,128)}) %reduce-scatter.13.cloned.1.call-update) | async-done | bytes 16777232 | tf_op jit(solution)/shard_map/while
  2812.8 17.1 select_add_fusion.5
  2829.9 0.7 all-gather.11.cloned.1.call-update
  2830.6 0.5 all-gather.13.cloned.1.call-update
  2831.3 200.3 %all-gather.11.cloned.1.call-done = bf16[1,2048,8192]{2,1,0:T(8,128)(2,1)} async-done(((bf16[1,512,8192]{2,1,0:T(8,128)(2,1)}), bf16[1,2048,8192]{2,1,0:T(8,128)(2,1)}) %all-gather.11.cloned.1.call-update) | async-done | bytes 33554448 | tf_op jit(solution)/shard_map/while/body/eval_jaxpr/all_gather | solution.py:8
  3031.6 41.8 fusion.78
  3073.4 158.9 %all-gather.13.cloned.1.call-done = bf16[1,8192,2048]{2,1,0:T(8,128)(2,1)} async-done(((bf16[1,2048,2048]{2,1,0:T(8,128)(2,1)}), bf16[1,8192,2048]{2,1,0:T(8,128)(2,1)}) %all-gather.13.cloned.1.call-update) | async-done | bytes 33554448 | tf_op jit(solution)/shard_map/while/body/eval_jaxpr/all_gather | solution.py:8
  3232.3 62.7 %fusion.79 = bf16[1024,8192]{1,0:T(8,128)(2,1)} fusion(bf16[1024,8192]{1,0:T(8,128)(2,1)} %fusion.78, bf16[1,8192,2048]{2,1,0:T(8,128)(2,1)} %all-gather.13.cloned.1.call-done, bf16[3,1024,2048]{2,1,0:T(8,128)(2,1)} %get-tuple-element.225, s32[]{:T(128)} %get-tuple-element.210, pred[1024]{0:T(1024)(128)(4,1)S(1)} %dynamic-slice_reduce_fusion.2), kind=kOutput, calls=%fused_computation.8.clone.clone.2.clone.1 | convolution fusion | flops 34537996288 | bytes 71304704 | tf_op jit(solution)/shard_map/while/body/eval_jaxpr/td,fd->tf/dot_general | solution.py:40
  3295.0 45.2 fusion.80
  3340.2 0.0 reduce-scatter.13.cloned.1.call-start
  3340.3 52.9 %fusion.81 = f32[8192,2048]{1,0:T(8,128)} fusion(bf16[1024,8192]{1,0:T(8,128)(2,1)} %fusion.78, bf16[3,1024,2048]{2,1,0:T(8,128)(2,1)} %get-tuple-element.225, s32[]{:T(128)} %get-tuple-element.210, pred[1024]{0:T(1024)(128)(4,1)S(1)} %dynamic-slice_reduce_fusion.2), kind=kOutput, calls=%fused_computation.19.clone.1 | convolution fusion | flops 34445721600 | bytes 88081920 | tf_op jit(solution)/shard_map/while/body/eval_jaxpr/tf,td->fd/dot_general | solution.py:42
  3393.2 387.7 %reduce-scatter.11.cloned.1.call-done = f32[512,8192]{1,0:T(8,128)} async-done(((f32[2048,8192]{1,0:T(8,128)}), f32[512,8192]{1,0:T(8,128)}) %reduce-scatter.11.cloned.1.call-update) | async-done | bytes 16777232 | tf_op jit(solution)/shard_map/while
  3780.9 17.9 select_add_fusion.4
  3798.8 425.1 %reduce-scatter.13.cloned.1.call-done = f32[2048,2048]{1,0:T(8,128)} async-done(((f32[8192,2048]{1,0:T(8,128)}), f32[2048,2048]{1,0:T(8,128)}) %reduce-scatter.13.cloned.1.call-update) | async-done | bytes 16777232 | tf_op jit(solution)/shard_map/while
  4223.9 17.1 select_add_fusion.5
  4242.2 0.0 all-reduce.5.cloned.1.call-start
  4242.2 0.5 all-reduce.5.cloned.1.call-update
  4242.8 734.7 %all-reduce.5.cloned.1.call-done = (f32[1,512,8192]{2,1,0:T(8,128)}, f32[1,2048,2048]{2,1,0:T(8,128)}) async-done(((f32[1,512,8192]{2,1,0:T(8,128)}, f32[1,2048,2048]{2,1,0:T(8,128)}), (f32[1,512,8192]{2,1,0:T(8,128)}, f32[1,2048,2048]{2,1,0:T(8,128)})) %all-reduce.5.cloned.1.call-update) | async-done | bytes 33554448 | tf_op jit(solution)/shard_map/psum | solution.py:54
  4977.5 12.5 copy.18
  4990.1 3.9 copy-done
  4993.9 6.2 copy.19
  (32 shorter events, 0.5 us)
Async XLA Ops:
  8.7 246.4 %copy-start.1 = (pred[3,1024]{1,0:T(4,128)(4,1)}, pred[3,1024]{1,0:T(4,128)(4,1)S(1)}, u32[]{:S(2)}) copy-start(pred[3,1024]{1,0:T(4,128)(4,1)S(1)} %get-tuple-element.224) | copy-start | bytes 9220 | tf_op jit(solution)/shard_map/while
  8.7 204.6 %all-gather.11.cloned.1.call-start = ((), (), s32[]{:S(2)}) async-start(), calls=%async_computation.3 | async-start | bytes 41943040 | tf_op jit(solution)/shard_map/while/body/eval_jaxpr/all_gather | solution.py:8
  9.5 404.7 %all-gather.13.cloned.1.call-start = ((), (), s32[]{:S(2)}) async-start(), calls=%async_computation.4 | async-start | bytes 41943040 | tf_op jit(solution)/shard_map/while/body/eval_jaxpr/all_gather | solution.py:8
  10.2 952.6 %reduce-scatter.11.cloned.1.call-start = ((), (), s32[]{:S(2)}) async-start(), calls=%async_computation.5 | async-start | bytes 83886080 | tf_op jit(solution)/shard_map/while
  522.1 883.7 %reduce-scatter.13.cloned.1.call-start = ((), (), s32[]{:S(2)}) async-start(), calls=%async_computation.6 | async-start | bytes 83886080 | tf_op jit(solution)/shard_map/while
  1405.8 13.1 copy-start.2
  1418.9 243.2 %copy-start.1 = (pred[3,1024]{1,0:T(4,128)(4,1)}, pred[3,1024]{1,0:T(4,128)(4,1)S(1)}, u32[]{:S(2)}) copy-start(pred[3,1024]{1,0:T(4,128)(4,1)S(1)} %get-tuple-element.224) | copy-start | bytes 9220 | tf_op jit(solution)/shard_map/while
  1418.9 201.4 %all-gather.11.cloned.1.call-start = ((), (), s32[]{:S(2)}) async-start(), calls=%async_computation.3 | async-start | bytes 41943040 | tf_op jit(solution)/shard_map/while/body/eval_jaxpr/all_gather | solution.py:8
  1419.5 401.6 %all-gather.13.cloned.1.call-start = ((), (), s32[]{:S(2)}) async-start(), calls=%async_computation.4 | async-start | bytes 41943040 | tf_op jit(solution)/shard_map/while/body/eval_jaxpr/all_gather | solution.py:8
  1420.1 949.6 %reduce-scatter.11.cloned.1.call-start = ((), (), s32[]{:S(2)}) async-start(), calls=%async_computation.5 | async-start | bytes 83886080 | tf_op jit(solution)/shard_map/while
  1929.0 883.8 %reduce-scatter.13.cloned.1.call-start = ((), (), s32[]{:S(2)}) async-start(), calls=%async_computation.6 | async-start | bytes 83886080 | tf_op jit(solution)/shard_map/while
  2812.8 17.1 copy-start.2
  2829.9 243.5 %copy-start.1 = (pred[3,1024]{1,0:T(4,128)(4,1)}, pred[3,1024]{1,0:T(4,128)(4,1)S(1)}, u32[]{:S(2)}) copy-start(pred[3,1024]{1,0:T(4,128)(4,1)S(1)} %get-tuple-element.224) | copy-start | bytes 9220 | tf_op jit(solution)/shard_map/while
  2829.9 201.7 %all-gather.11.cloned.1.call-start = ((), (), s32[]{:S(2)}) async-start(), calls=%async_computation.3 | async-start | bytes 41943040 | tf_op jit(solution)/shard_map/while/body/eval_jaxpr/all_gather | solution.py:8
  2830.6 401.7 %all-gather.13.cloned.1.call-start = ((), (), s32[]{:S(2)}) async-start(), calls=%async_computation.4 | async-start | bytes 41943040 | tf_op jit(solution)/shard_map/while/body/eval_jaxpr/all_gather | solution.py:8
  2831.2 949.7 %reduce-scatter.11.cloned.1.call-start = ((), (), s32[]{:S(2)}) async-start(), calls=%async_computation.5 | async-start | bytes 83886080 | tf_op jit(solution)/shard_map/while
  3340.2 883.7 %reduce-scatter.13.cloned.1.call-start = ((), (), s32[]{:S(2)}) async-start(), calls=%async_computation.6 | async-start | bytes 83886080 | tf_op jit(solution)/shard_map/while
  4223.9 17.1 copy-start.2
  4242.2 735.3 %all-reduce.5.cloned.1.call-start = ((), (), s32[]{:S(2)}) async-start(), calls=%async_computation.2 | async-start | bytes 67108864 | tf_op jit(solution)/shard_map/psum | solution.py:54
  4977.5 16.4 copy-start
Sparse Core Ops, SparseCore 0:
  11.1 202.1 all-gather.10
  214.8 199.3 all-gather.12
  522.2 440.5 reduce-scatter.10
  965.2 440.5 reduce-scatter.12
  1420.9 199.3 all-gather.10
  1621.7 199.3 all-gather.12
  1929.1 440.5 reduce-scatter.10
  2372.2 440.5 reduce-scatter.12
  2832.2 199.3 all-gather.10
  3033.0 199.3 all-gather.12
  3340.4 440.5 reduce-scatter.10
  3783.3 440.5 reduce-scatter.12
Sparse Core Ops, SparseCore 1:
  4245.7 731.7 all-reduce.4
where the time goes:
time: 5030 us; the launch traced here: 5010 us
  waiting for transfers between devices  4260 us (85%)
  matrix products  608 us (12%)
  other arithmetic  95.6 us (2%)
    while x18, waiting for transfers between devices  2450 us
    all_gather x6, waiting for transfers between devices, gather_full(): return lax.all_gather(w_shard, 'fsdp', axis=0, tiled=True)  1080 us
    psum x1, waiting for transfers between devices, device_grads(): grad_up = lax.psum(jnp.stack(acc_up), 'replica')  735 us
    dot_general x3, matrix products, micro_step(): jnp.einsum('td,fd->tf', grad_x, down_full, preferred_element_type=jnp.flo...  188 us
    dot_general x3, matrix products, micro_step(): jnp.einsum('tf,td->fd', act_bf, grad_x, preferred_element_type=jnp.float32)  159 us
    dot_general x3, matrix products, micro_step(): jnp.einsum('td,tf->df', x_prev, grad_hid, preferred_element_type=jnp.floa...  135 us
    dot_general x3, matrix products, micro_step(): jnp.dot(x_cur, up_full, preferred_element_type=jnp.float32)  125 us
  transfers between devices with their start and end apart: 13, of which 13 were waited for; matrix products, arithmetic and copies ran while one was open for 7% of the time, Pallas kernels for 0%

commit v1 on v0

v1 whole, which is shorter than its diff:
```python
import jax
import jax.numpy as jnp
from jax import lax
from jax.experimental import pallas as pl
from jax.experimental.pallas import tpu as pltpu
from jax.sharding import PartitionSpec as P


D = 2048
TOK = 1024
MICRO = 3
BASE = 256
REST = TOK - BASE
TM = 128
NT = MICRO * REST // TM
RROWS = MICRO * REST + TM
CAP = 6
G = 4
M = G * TM
FB = 256
HB = FB // 2
NCH = D // FB
HALF = 1024
NSRC = 12
C1 = 0.7978845608028654
C3 = 0.044715
BF = jnp.bfloat16
F32 = jnp.float32


ANY = pl.BlockSpec(memory_space=pl.ANY)
SM = pl.BlockSpec(memory_space=pltpu.SMEM)
VM = pl.BlockSpec(memory_space=pltpu.VMEM)
MIB = 1024 * 1024

CORE = [(0, 1), (1, 0), (2, 3), (3, 2)]
XSWAP = [(0, 2), (2, 0), (1, 3), (3, 1)]
XDIAG = [(0, 3), (3, 0), (1, 2), (2, 1)]
YSWAP = [(0, 1), (1, 0)]
YDIAG = [(r * 4 + f, (1 - r) * 4 + (f ^ 1)) for r in range(2) for f in range(4)]


def core_swap(v):
    return lax.ppermute(v, "fsdp", CORE)


def x_swap(v):
    return lax.ppermute(v, "fsdp", XSWAP)


def x_diag(v):
    return lax.ppermute(v, "fsdp", XDIAG)


def y_swap(v):
    return lax.ppermute(v, "replica", YSWAP)


def y_diag(v):
    return lax.ppermute(v, ("replica", "fsdp"), YDIAG)


def cost(flops, nbytes):
    return pl.CostEstimate(flops=flops, bytes_accessed=nbytes, transcendentals=0)


def pack_rest(x_in, dy, rest, offs):
    def kern(rest_ref, offs_ref, x_ref, d_ref, out_ref, buf, zero, isem, osem, zsem):
        loads = []
        for k in range(MICRO):
            for a, ref in enumerate((x_ref, d_ref)):
                cp = pltpu.make_async_copy(ref.at[k, pl.ds(BASE, REST), :], buf.at[k, a], isem.at[k, a])
                cp.start()
                loads.append(cp)
        zero[...] = jnp.zeros_like(zero)
        for k in range(MICRO):
            n = rest_ref[k]
            for a in range(2):
                loads[2 * k + a].wait()
                for r in range(0, REST, TM):
                    row = lax.broadcasted_iota(jnp.int32, (TM, D), 0) + r
                    blk = buf[k, a, r : r + TM, :]
                    buf[k, a, r : r + TM, :] = jnp.where(row < n, blk, jnp.zeros_like(blk))
            o = pl.multiple_of(offs_ref[k], 16)
            cps = [
                pltpu.make_async_copy(buf.at[k, a], out_ref.at[a, pl.ds(o, REST), :], osem.at[a]) for a in range(2)
            ]
            for cp in cps:
                cp.start()
            for cp in cps:
                cp.wait()
        for o in (pl.multiple_of(offs_ref[MICRO], 16), MICRO * REST):
            cps = [pltpu.make_async_copy(zero, out_ref.at[a, pl.ds(o, TM), :], zsem.at[a]) for a in range(2)]
            for cp in cps:
                cp.start()
            for cp in cps:
                cp.wait()

    return pl.pallas_call(
        kern,
        in_specs=[SM, SM, ANY, ANY],
        out_specs=ANY,
        out_shape=jax.ShapeDtypeStruct((2, RROWS, D), BF),
        scratch_shapes=[
            pltpu.VMEM((MICRO, 2, REST, D), BF),
            pltpu.VMEM((TM, D), BF),
            pltpu.SemaphoreType.DMA((MICRO, 2)),
            pltpu.SemaphoreType.DMA((2,)),
            pltpu.SemaphoreType.DMA((2,)),
        ],
        compiler_params=pltpu.CompilerParams(vmem_limit_bytes=40 * MIB),
        cost_estimate=cost(15_000_000_000, 50_000_000),
        name="pack_rest",
    )(rest, offs, x_in, dy)


def build_send(own, sib, info):
    def kern(info_ref, own_ref, sib_ref, out_ref, buf, isem, osem):
        n, mine, shift = info_ref[0], info_ref[1], info_ref[2]

        def load(i, slot):
            @pl.when(i < mine)
            def _():
                r = pl.multiple_of(i * TM, TM)
                pltpu.make_async_copy(own_ref.at[:, pl.ds(r, TM), :], buf.at[slot], isem.at[slot]).start()

            @pl.when(i >= mine)
            def _():
                r = pl.multiple_of((i + shift) * TM, TM)
                pltpu.make_async_copy(sib_ref.at[:, pl.ds(r, TM), :], buf.at[slot], isem.at[slot]).start()

        def store(i, slot):
            r = pl.multiple_of(i * TM, TM)
            return pltpu.make_async_copy(buf.at[slot], out_ref.at[:, pl.ds(r, TM), :], osem.at[slot])

        for s in range(3):

            @pl.when(s < n)
            def _():
                load(s, s)

        def body(i, _):
            slot = lax.rem(i, 4)
            pltpu.make_async_copy(own_ref.at[:, pl.ds(0, TM), :], buf.at[slot], isem.at[slot]).wait()
            store(i, slot).start()

            @pl.when(i >= 1)
            def _():
                store(i - 1, lax.rem(i + 3, 4)).wait()

            @pl.when(i + 3 < n)
            def _():
                load(i + 3, lax.rem(i + 3, 4))

            return 0

        lax.fori_loop(0, n, body, 0)

        @pl.when(n > 0)
        def _():
            store(n - 1, lax.rem(n + 3, 4)).wait()

    return pl.pallas_call(
        kern,
        in_specs=[SM, ANY, ANY],
        out_specs=ANY,
        out_shape=jax.ShapeDtypeStruct((2, NT * TM, D), BF),
        scratch_shapes=[pltpu.VMEM((4, 2, TM, D), BF), pltpu.SemaphoreType.DMA((4,)), pltpu.SemaphoreType.DMA((4,))],
        cost_estimate=cost(10_000_000_000, 36_000_000),
        name="build_send",
    )(info, own, sib)


def gelu_and_slope(u):
    u2 = u * u
    t = jnp.tanh(u * (C1 + (C1 * C3) * u2))
    half = 0.5 + 0.5 * t
    act = u * half
    slope = half + (0.5 * u) * (1.0 - t * t) * (C1 + (3 * C1 * C3) * u2)
    return act, slope


def chunk_grads(j, tab, info, srcs, wus, wds, deps):
    def kern(tab_ref, info_ref, *refs):
        src = refs[:NSRC]
        wu_refs, wd_refs = refs[NSRC : NSRC + 4], refs[NSRC + 4 : NSRC + 6]
        refs = refs[NSRC + 6 + len(deps) :]
        keep_d, keep_u, send, xb, db, wub, wdb, gd, gu, sem, wsem, osem = refs
        groups, xi, f = info_ref[0], info_ref[1], info_ref[2]
        c0 = j * HB
        wcp = []
        for a in range(2):
            for k in range(4):
                rows = pl.ds(pl.multiple_of((f ^ k) * 512, 512), 512)
                wcp.append(
                    pltpu.make_async_copy(
                        wu_refs[k].at[a, :, pl.ds(c0, HB)], wub.at[rows, pl.ds(a * HB, HB)], wsem.at[k, a]
                    )
                )
            wcp.append(
                pltpu.make_async_copy(wd_refs[a].at[pl.ds(c0, HB), :], wdb.at[pl.ds(a * HB, HB), :], wsem.at[4, a])
            )
        for cp in wcp:
            cp.start()

        def pick(e, lo, hi, fn):
            if hi - lo == 1:
                fn(lo)
                return
            mid = (lo + hi) // 2

            @pl.when(e < mid * 32)
            def _():
                pick(e, lo, mid, fn)

            @pl.when(e >= mid * 32)
            def _():
                pick(e, mid, hi, fn)

        def issue(g, slot):
            for s in range(G):
                e = tab_ref[g * G + s]
                r = pl.multiple_of(lax.rem(e, 32) * TM, TM)

                def fetch(k):
                    rows = pl.ds(s * TM, TM)
                    pltpu.make_async_copy(src[k].at[0, pl.ds(r, TM), :], xb.at[slot, rows, :], sem.at[slot, 0]).start()
                    pltpu.make_async_copy(src[k].at[1, pl.ds(r, TM), :], db.at[slot, rows, :], sem.at[slot, 1]).start()

                pick(e, 0, NSRC, fetch)

        issue(0, 0)
        gd[...] = jnp.zeros_like(gd)
        gu[...] = jnp.zeros_like(gu)
        for cp in wcp:
            cp.wait()

        def body(g, _):
            slot = lax.rem(g, 2)

            @pl.when(g + 1 < groups)
            def _():
                issue(g + 1, 1 - slot)

            pltpu.make_async_copy(xb.at[slot], xb.at[slot], sem.at[slot, 0]).wait()
            pltpu.make_async_copy(db.at[slot], db.at[slot], sem.at[slot, 1]).wait()
            x, dy = xb[slot], db[slot]
            u = jnp.dot(x, wub[...], preferred_element_type=F32).astype(BF).astype(F32)
            da = lax.dot_general(dy, wdb[...], (((1,), (1,)), ((), ())), preferred_element_type=F32)
            act, slope = gelu_and_slope(u)
            dh = (da * slope).astype(BF)
            gd[...] += lax.dot_general(act.astype(BF), dy, (((0,), (0,)), ((), ())), preferred_element_type=F32)
            gu[...] += lax.dot_general(dh, x, (((0,), (0,)), ((), ())), preferred_element_type=F32)
            return 0

        lax.fori_loop(0, groups, body, 0)
        kc = pl.multiple_of(xi * HALF, HALF)
        sc = pl.multiple_of((1 - xi) * HALF, HALF)
        ocp = [
            (gd.at[pl.ds(HB, HB), :], send.at[pl.ds(0, HB), :]),
            (gu.at[pl.ds(0, HB), pl.ds(sc, HALF)], send.at[pl.ds(HB, HB), pl.ds(0, HALF)]),
            (gu.at[pl.ds(HB, HB), pl.ds(sc, HALF)], send.at[pl.ds(HB, HB), pl.ds(HALF, HALF)]),
            (gd.at[pl.ds(0, HB), :], keep_d),
            (gu.at[:, pl.ds(kc, HALF)], keep_u),
        ]
        ocp = [pltpu.make_async_copy(a, b, osem.at[i]) for i, (a, b) in enumerate(ocp)]
        for cp in ocp:
            cp.start()
        for cp in ocp:
            cp.wait()

    n_in = NSRC + 6 + len(deps)
    return pl.pallas_call(
        kern,
        in_specs=[SM, SM] + [ANY] * n_in,
        out_specs=[ANY] * 3,
        out_shape=[
            jax.ShapeDtypeStruct((HB, D), F32),
            jax.ShapeDtypeStruct((FB, HALF), F32),
            jax.ShapeDtypeStruct((FB, D), F32),
        ],
        scratch_shapes=[
            pltpu.VMEM((2, M, D), BF),
            pltpu.VMEM((2, M, D), BF),
            pltpu.VMEM((D, FB), BF),
            pltpu.VMEM((FB, D), BF),
            pltpu.VMEM((FB, D), F32),
            pltpu.VMEM((FB, D), F32),
            pltpu.SemaphoreType.DMA((2, 2)),
            pltpu.SemaphoreType.DMA((5, 2)),
            pltpu.SemaphoreType.DMA((5,)),
        ],
        compiler_params=pltpu.CompilerParams(vmem_limit_bytes=40 * MIB),
        cost_estimate=cost(8 * 8192 * D * FB, 70_000_000),
    )(tab, info, *srcs, *wus, *wds, *deps)


def finish(j, pos, keep_d, keep_u, recv, outs):
    first = outs is None

    def kern(pos_ref, kd, ku, rc, *refs):
        refs = refs if first else refs[2:]
        out_d, out_u, fd, fuc, fus, vd, vu, sem = refs
        y, xi, c = pos_ref[0], pos_ref[1], pos_ref[2]
        vd[...] = kd[...] + rc[0:HB, :]
        row = pl.multiple_of(y * HALF + j * HB, HB)
        cps = [
            pltpu.make_async_copy(vd, fd, sem.at[0]),
            pltpu.make_async_copy(vd, out_d.at[pl.ds(row, HB), :], sem.at[1]),
        ]
        for cp in cps:
            cp.start()
        vu[0] = (ku[0:HB, :] + rc[HB:FB, HALF:D]).T
        vu[1] = (ku[HB:FB, :] + rc[HB:FB, 0:HALF]).T
        mine = pl.ds(pl.multiple_of(c * 512, 512), 512)
        other = pl.ds(pl.multiple_of((1 - c) * 512, 512), 512)
        more = [
            pltpu.make_async_copy(vu.at[:, other, :], fus, sem.at[2]),
            pltpu.make_async_copy(vu.at[:, mine, :], fuc, sem.at[3]),
        ]
        for a in range(2):
            xa = xi if a == 0 else 1 - xi
            col = pl.multiple_of(((2 * xa + c) * 2 + y) * HALF + j * HB, HB)
            more.append(pltpu.make_async_copy(vu.at[a, mine, :], out_u.at[:, pl.ds(col, HB)], sem.at[4 + a]))
        for cp in more:
            cp.start()
        for cp in cps + more:
            cp.wait()

    shapes = [
        jax.ShapeDtypeStruct((D, D), F32),
        jax.ShapeDtypeStruct((512, 4 * D), F32),
        jax.ShapeDtypeStruct((HB, D), F32),
        jax.ShapeDtypeStruct((2, 512, HB), F32),
        jax.ShapeDtypeStruct((2, 512, HB), F32),
    ]
    extra = [] if first else list(outs)
    return pl.pallas_call(
        kern,
        in_specs=[SM, VM, VM, VM] + [ANY] * len(extra),
        out_specs=[ANY] * 5,
        out_shape=shapes,
        scratch_shapes=[pltpu.VMEM((HB, D), F32), pltpu.VMEM((2, HALF, HB), F32), pltpu.SemaphoreType.DMA((6,))],
        input_output_aliases={} if first else {4: 0, 5: 1},
        compiler_params=pltpu.CompilerParams(vmem_limit_bytes=24 * MIB),
        cost_estimate=cost(4_000_000_000, 9_000_000),
    )(pos, keep_d, keep_u, recv, *extra)


def store(j, pos, rd, ruc, ruy, rus, outs):
    def kern(pos_ref, d_ref, uc_ref, uy_ref, us_ref, _d, _u, out_d, out_u, vd, vu, isem, osem):
        y, xi, c = pos_ref[0], pos_ref[1], pos_ref[2]
        loads = [pltpu.make_async_copy(d_ref, vd, isem.at[0])]
        for k, r in enumerate((uc_ref, uy_ref, us_ref)):
            loads.append(pltpu.make_async_copy(r, vu.at[k], isem.at[1 + k]))
        for cp in loads:
            cp.start()
        row = pl.multiple_of((1 - y) * HALF + j * HB, HB)
        loads[0].wait()
        outc = [pltpu.make_async_copy(vd, out_d.at[pl.ds(row, HB), :], osem.at[0])]
        outc[0].start()
        for k, (cc, yy) in enumerate(((c, 1 - y), (1 - c, 1 - y), (1 - c, y))):
            loads[1 + k].wait()
            for a in range(2):
                xa = xi if a == 0 else 1 - xi
                col = pl.multiple_of(((2 * xa + cc) * 2 + yy) * HALF + j * HB, HB)
                cp = pltpu.make_async_copy(vu.at[k, a], out_u.at[:, pl.ds(col, HB)], osem.at[1 + 2 * k + a])
                cp.start()
                outc.append(cp)
        for cp in outc:
            cp.wait()

    return pl.pallas_call(
        kern,
        in_specs=[SM] + [ANY] * 6,
        out_specs=[ANY] * 2,
        out_shape=[jax.ShapeDtypeStruct((D, D), F32), jax.ShapeDtypeStruct((512, 4 * D), F32)],
        scratch_shapes=[
            pltpu.VMEM((HB, D), F32),
            pltpu.VMEM((3, 2, 512, HB), F32),
            pltpu.SemaphoreType.DMA((4,)),
            pltpu.SemaphoreType.DMA((7,)),
        ],
        input_output_aliases={5: 0, 6: 1},
        compiler_params=pltpu.CompilerParams(vmem_limit_bytes=16 * MIB),
        cost_estimate=cost(3_000_000_000, 5_000_000),
    )(pos, rd, ruc, ruy, rus, *outs)


def exchange_branch(n):
    def run(send, s1_y):
        s1_ys = core_swap(s1_y)
        mine, sibs = [], []
        for p in range(NT // CAP):
            k = min(max(n - p * CAP, 0), CAP)
            if k == 0:
                got = jnp.zeros((2, CAP * TM, D), BF)
                mine.append(got)
                sibs.append(got)
                continue
            got = y_swap(send[:, p * CAP * TM : (p * CAP + k) * TM, :])
            sib = core_swap(got)
            if k < CAP:
                pad = ((0, 0, 0), (0, (CAP - k) * TM, 0), (0, 0, 0))
                got = lax.pad(got, jnp.zeros((), BF), pad)
                sib = lax.pad(sib, jnp.zeros((), BF), pad)
            mine.append(got)
            sibs.append(sib)
        return (s1_ys, *mine, *sibs)

    return run


def solution(mesh):
    tok_spec = P(None, ("model", "replica", "fsdp"), None)
    len_spec = P(None, ("model", "replica", "fsdp"))
    w_spec = P(None, ("model", "fsdp"), None)

    def group_grads(x_in, dy, lengths, w_up, w_down):
        y, f = lax.axis_index("replica"), lax.axis_index("fsdp")
        xi, c = f // 2, f % 2
        w_up, w_down = w_up[0], w_down[0]

        s1 = jnp.stack([x_in[:, :BASE], dy[:, :BASE]]).reshape(2, MICRO * BASE, D)
        s1_y = y_swap(s1)

        def cols(xd, cd):
            own = lax.dynamic_slice(w_up, (0, ((2 * xd + cd) * 2 + y) * HALF), (512, HALF))
            oth = lax.dynamic_slice(w_up, (0, ((2 * (1 - xd) + cd) * 2 + y) * HALF), (512, HALF))
            return jnp.stack([own, oth])

        wd_own = lax.dynamic_slice(w_down, (y * HALF, 0), (HALF, D))
        from_x = x_swap(cols(1 - xi, c))
        from_d = x_diag(cols(1 - xi, 1 - c))
        wd_oth = x_swap(wd_own)
        from_s = core_swap(cols(xi, 1 - c))
        wus = (cols(xi, c), from_s, from_x, from_d)
        wds = (wd_own, wd_oth)

        lens = lax.all_gather(lengths[:, 0], ("replica", "fsdp")).astype(jnp.int32)
        rest = lens - BASE
        r16 = (rest + 15) // 16 * 16
        tiles = (jnp.sum(r16, axis=1) + TM - 1) // TM
        me = y * 4 + f
        my_rest = lax.dynamic_index_in_dim(rest, me, keepdims=False)
        my16 = lax.dynamic_index_in_dim(r16, me, keepdims=False)
        offs = jnp.concatenate([jnp.zeros((1,), jnp.int32), jnp.cumsum(my16)])
        both = tiles[0::2] + tiles[1::2]
        share = jnp.stack([(both + 1) // 2, both // 2], axis=1).reshape(8)
        n2 = jnp.max(share)

        def at(v, i):
            return lax.dynamic_index_in_dim(v, i, keepdims=False)

        t_own, t_sib = at(tiles, me), at(tiles, me ^ 1)
        h_own = at(share, me)
        h_y, h_ys = at(share, me ^ 4), at(share, me ^ 5)

        packed = pack_rest(x_in, dy, my_rest, offs)
        packed_s = core_swap(packed)
        s1_s = core_swap(s1)
        send2 = build_send(packed, packed_s, jnp.stack([h_own, t_own, t_sib - h_own]))

        i = jnp.arange(128)
        b1 = 24
        b2 = b1 + t_own
        b3 = b2 + t_sib
        b4 = b3 + h_y
        b5 = b4 + h_ys
        k3, k4 = i - b3, i - b4
        tab = jnp.where(i < b5, (9 + k4 // CAP) * 32 + k4 % CAP, 4 * 32 + NT)
        tab = jnp.where(i < b4, (6 + k3 // CAP) * 32 + k3 % CAP, tab)
        tab = jnp.where(i < b3, 5 * 32 + (i - b2), tab)
        tab = jnp.where(i < b2, 4 * 32 + (i - b1), tab)
        tab = jnp.where(i < b1, (i // 6) * 32 + i % 6, tab).astype(jnp.int32)
        info = jnp.stack([(b5 + G - 1) // G, xi, f]).astype(jnp.int32)
        pos = jnp.stack([y, xi, c]).astype(jnp.int32)

        s1_ys, *s2 = lax.switch(n2, [exchange_branch(n) for n in range(NT + 1)], send2, s1_y)
        srcs = (s1, s1_s, s1_y, s1_ys, packed, packed_s, *s2)

        outs = None
        fin = []
        for j in range(NCH):
            deps = (fin[j - 2][0],) if j >= 2 else ()
            keep_d, keep_u, send = chunk_grads(j, tab, info, srcs, wus, wds, deps)
            recv = x_swap(send)
            *outs, fd, fuc, fus = finish(j, pos, keep_d, keep_u, recv, outs)
            rd = y_swap(fd)
            ruc = y_swap(fuc)
            ruy = y_diag(fus)
            rus = core_swap(fus)
            fin.append((fd, (rd, ruc, ruy, rus)))
            if j >= 2:
                outs = store(j - 2, pos, *fin[j - 2][1], outs)
        for j in range(NCH - 2, NCH):
            outs = store(j, pos, *fin[j][1], outs)
        return outs[1][None], outs[0][None]

    return jax.shard_map(
        group_grads,
        mesh=mesh,
        in_specs=(tok_spec, tok_spec, len_spec, w_spec, w_spec),
        out_specs=(w_spec, w_spec),
        check_vma=False,
    )
```

time: 5030 us -> 1430 us (0.28)
  waiting for transfers between devices: 4260 us -> 797 us
  matrix products: 608 us -> 0 us
  Pallas kernels: 0 us -> 495 us
  other arithmetic: 95.6 us -> 10.4 us
    while x18 -> x0, waiting for transfers between devices: 2450 us -> none
    all_gather x6 -> x0, waiting for transfers between devices: 1080 us -> none  [gather_full(): return lax.all_gather(w_shard, 'fsdp', axis=0, tiled=True)]
    ppermute x0 -> x54, waiting for transfers between devices: none -> 797 us  [the longest x20 584 us: y_swap(): return lax.ppermute(v, 'replica', YSWAP)]
    psum x1 -> x0, waiting for transfers between devices: 735 us -> none  [device_grads(): grad_up = lax.psum(jnp.stack(acc_up), 'replica')]
    dot_general x12 -> x0, matrix products: 608 us -> none  [the longest x3 188 us: micro_step(): jnp.einsum('td,fd->tf', grad_x, down_full, preferred_element_type=jnp.flo...]
    pallas_call x0 -> x26, Pallas kernels: none -> 495 us  [the longest x8 435 us: chunk_grads(): pl.pallas_call(kern, in_specs=[SM, SM] + [ANY] * n_in, out_specs=[ANY] *...]
    add x6 -> x0, other arithmetic: 94.8 us -> none  [the longest x3 47.6 us: micro_step(): new_up[layer_idx]]
  transfers between devices with their start and end apart: 13 -> 54, of which waited for: 13 -> 14; matrix products, arithmetic and copies ran while one was open for 7% -> 2% of each run, Pallas kernels for 0% -> 30%
where the time goes in v1:
time: 1430 us; the launch traced here: 1420 us
  waiting for transfers between devices  797 us (56%)
  Pallas kernels  495 us (35%)
  local copies, waits for them, and re-layouts  34.8 us (2%)
  starting transfers between devices  34 us (2%)
  blocking collectives  25 us (2%)
  loops' own time  17 us (1%)
    ppermute x20, waiting for transfers between devices, y_swap(): return lax.ppermute(v, 'replica', YSWAP)  584 us
    pallas_call x8, Pallas kernels, chunk_grads(): pl.pallas_call(kern, in_specs=[SM, SM] + [ANY] * n_in, out_specs=[ANY] *...  435 us
    ppermute x10, waiting for transfers between devices, x_swap(): return lax.ppermute(v, 'fsdp', XSWAP)  126 us
    ppermute x1, waiting for transfers between devices, x_diag(): return lax.ppermute(v, 'fsdp', XDIAG)  44 us
    ppermute x8, waiting for transfers between devices, y_diag(): return lax.ppermute(v, ('replica', 'fsdp'), YDIAG)  32.2 us
  transfers between devices with their start and end apart: 54, of which 14 were waited for; matrix products, arithmetic and copies ran while one was open for 2% of the time, Pallas kernels for 30%

profile of v1, /device:TPU:0, one launch (start us, length us, event | category | flops | bytes accessed | tf_op | source)
XLA Modules:
  0.0 1419.7 jit_solution(15809840568574574060)
XLA Ops:
  1.4 25.0 %all-reduce.30 = s32[24]{0:T(128)S(1)} all-reduce(s32[24]{0:T(128)S(1)} %bitcast_dynamic-update-slice_fusion), channel_id=2, replica_groups=mesh['model'=1,'replica'=2,'fsdp'=4] {'replica','fsdp'}, use_global_device_ids=true, to_apply=%add.30 | all-reduce | flops 24 | bytes 192
  27.0 4.6 copy-done
  31.5 14.1 pack_rest.1.own_ref.refs_4_
  48.5 3.1 pad_maximum_fusion.refs_0_
  51.6 2.2 collective-permute-start.92
  60.8 4.8 dynamic-slice_bitcast_fusion.refs_16_
  65.5 10.1 collective-permute-done.93.sib_ref.refs_5_
  75.7 9.0 build_send.1
  84.7 103.5 %collective-permute-done.92.refs_2_ = bf16[2,768,2048]{2,1,0:T(8,128)(2,1)} collective-permute-done((bf16[2,768,2048]{2,1,0:T(8,128)(2,1)}, bf16[2,768,2048]{2,1,0:T(8,128)(2,1)}, u32[]{:S(2)}, u32[]{:S(2)}) %collective-permute-start.92) | collective-permute-done | bytes 6291488 | tf_op jit(solution)/shard_map/ppermute | solution.py:56
  188.2 326.6 %conditional.1 = (bf16[2,768,2048]{2,1,0:T(8,128)(2,1)}, bf16[2,768,2048]{2,1,0:T(8,128)(2,1)}, bf16[2,768,2048]{2,1,0:T(8,128)(2,1)}, bf16[2,768,2048]{2,1,0:T(...) conditional(s32[]{:T(128)} %clamp.3, ...), branch_computations={%region_4.5_spmd, %region_5.6_spmd, %region_6.7_spmd, %region_7.8_... | conditional | bytes 226492736 | solution.py:479
  196.8 5.7 fusion.14
  204.5 136.5 %collective-permute-done.50 = bf16[2,768,2048]{2,1,0:T(8,128)(2,1)} collective-permute-done((bf16[2,768,2048]{2,1,0:T(8,128)(2,1)S(1)}, bf16[2,768,2048]{2,1,0:T(8,128)(2,1)}, u32[]{:S(2)}, u32[]{:S(2)}) %collective-permute-start.50) | collective-permute-done | bytes 6291488 | tf_op jit(solution)/shard_map/cond/branch_13_fun/ppermute | solution.py:56
  341.0 131.7 %collective-permute-done.51 = bf16[2,768,2048]{2,1,0:T(8,128)(2,1)} collective-permute-done((bf16[2,768,2048]{2,1,0:T(8,128)(2,1)S(1)}, bf16[2,768,2048]{2,1,0:T(8,128)(2,1)}, u32[]{:S(2)}, u32[]{:S(2)}) %collective-permute-start.51) | collective-permute-done | bytes 6291488 | tf_op jit(solution)/shard_map/cond/branch_13_fun/ppermute | solution.py:56
  474.7 24.8 %collective-permute-done.52 = bf16[2,128,2048]{2,1,0:T(8,128)(2,1)S(1)} collective-permute-done((bf16[2,128,2048]{2,1,0:T(8,128)(2,1)S(1)}, bf16[2,128,2048]{2,1,0:T(8,128)(2,1)S(1)}, u32[]{:S(2)}, u32[]{:S(2)}) %collective-permute-start.52) | collective-permute-done | bytes 1048608 | tf_op jit(solution)/shard_map/cond/branch_13_fun/ppermute | solution.py:56
  499.5 3.4 pad.80
  502.9 3.4 pad.81
  516.2 2.6 constant_dynamic-slice_fusion.1
  518.9 2.4 pad_maximum_fusion.4
  527.6 125.9 %collective-permute-done.95.refs_14_ = bf16[2,512,1024]{2,1,0:T(8,128)(2,1)} collective-permute-done((bf16[2,512,1024]{2,1,0:T(8,128)(2,1)}, bf16[2,512,1024]{2,1,0:T(8,128)(2,1)}, u32[]{:S(2)}, u32[]{:S(2)}) %collective-permute-start.95) | collective-permute-done | bytes 2097184 | tf_op jit(solution)/shard_map/ppermute | solution.py:48
  653.5 44.0 %collective-permute-done.96.refs_15_ = bf16[2,512,1024]{2,1,0:T(8,128)(2,1)} collective-permute-done((bf16[2,512,1024]{2,1,0:T(8,128)(2,1)}, bf16[2,512,1024]{2,1,0:T(8,128)(2,1)}, u32[]{:S(2)}, u32[]{:S(2)}) %collective-permute-start.96) | collective-permute-done | bytes 2097184 | tf_op jit(solution)/shard_map/ppermute | solution.py:52
  697.5 53.6 %shard_map.69 = (f32[128,2048]{1,0:T(8,128)S(1)}, f32[256,1024]{1,0:T(8,128)S(1)}, f32[256,2048]{1,0:T(8,128)S(1)}) custom-call(s32[128]{0:T(128)S(1)} %compare_select_fusion.4.tab_ref, s32[3]{0:T(128)S(1)} %pad_add_fusion.2.info_ref, bf16[2,768,2048]{2,1,0:T(8,128)(2,1)} %pad_maximum_fusion.refs_0_, bf16[2,768,2048]{2,1,0:T(8,128)(2,1)} %collective-permute-done.91.refs_1_, ...), custom_call_target="tpu_custom_call" | custom-call | flops 34359738368 | bytes 70000000 | tf_op jit(solution)/shard_map/pallas_call | solution.py:273
  751.2 53.6 %shard_map.68 = (f32[128,2048]{1,0:T(8,128)S(1)}, f32[256,1024]{1,0:T(8,128)S(1)}, f32[256,2048]{1,0:T(8,128)S(1)}) custom-call(s32[128]{0:T(128)S(1)} %compare_select_fusion.4.tab_ref, s32[3]{0:T(128)S(1)} %pad_add_fusion.2.info_ref, bf16[2,768,2048]{2,1,0:T(8,128)(2,1)} %pad_maximum_fusion.refs_0_, bf16[2,768,2048]{2,1,0:T(8,128)(2,1)} %collective-permute-done.91.refs_1_, ...), custom_call_target="tpu_custom_call" | custom-call | flops 34359738368 | bytes 70000000 | tf_op jit(solution)/shard_map/pallas_call | solution.py:273
  804.8 2.6 shard_map.70
  810.4 54.9 %shard_map.73 = (f32[128,2048]{1,0:T(8,128)S(1)}, f32[256,1024]{1,0:T(8,128)S(1)}, f32[256,2048]{1,0:T(8,128)}) custom-call(s32[128]{0:T(128)S(1)} %compare_select_fusion.4.tab_ref, s32[3]{0:T(128)S(1)} %pad_add_fusion.2.info_ref, bf16[2,768,2048]{2,1,0:T(8,128)(2,1)} %pad_maximum_fusion.refs_0_, bf16[2,768,2048]{2,1,0:T(8,128)(2,1)} %collective-permute-done.91.refs_1_, ...), custom_call_target="tpu_custom_call" | custom-call | flops 34359738368 | bytes 70000000 | tf_op jit(solution)/shard_map/pallas_call | solution.py:273
  867.1 2.6 shard_map.71
  870.6 54.6 %shard_map.72 = (f32[128,2048]{1,0:T(8,128)S(1)}, f32[256,1024]{1,0:T(8,128)S(1)}, f32[256,2048]{1,0:T(8,128)}) custom-call(s32[128]{0:T(128)S(1)} %compare_select_fusion.4.tab_ref, s32[3]{0:T(128)S(1)} %pad_add_fusion.2.info_ref, bf16[2,768,2048]{2,1,0:T(8,128)(2,1)} %pad_maximum_fusion.refs_0_, bf16[2,768,2048]{2,1,0:T(8,128)(2,1)} %collective-permute-done.91.refs_1_, ...), custom_call_target="tpu_custom_call" | custom-call | flops 34359738368 | bytes 70000000 | tf_op jit(solution)/shard_map/pallas_call | solution.py:273
  925.3 2.5 shard_map.74
  927.8 54.7 %shard_map.78 = (f32[128,2048]{1,0:T(8,128)S(1)}, f32[256,1024]{1,0:T(8,128)S(1)}, f32[256,2048]{1,0:T(8,128)}) custom-call(s32[128]{0:T(128)S(1)} %compare_select_fusion.4.tab_ref, s32[3]{0:T(128)S(1)} %pad_add_fusion.2.info_ref, bf16[2,768,2048]{2,1,0:T(8,128)(2,1)} %pad_maximum_fusion.refs_0_, bf16[2,768,2048]{2,1,0:T(8,128)(2,1)} %collective-permute-done.91.refs_1_, ...), custom_call_target="tpu_custom_call" | custom-call | flops 34359738368 | bytes 70000000 | tf_op jit(solution)/shard_map/pallas_call | solution.py:273
  985.1 2.3 shard_map.75
  989.1 2.5 shard_map.76
  991.6 39.7 %collective-permute-done.113.uc_ref = f32[2,512,128]{2,1,0:T(8,128)S(1)} collective-permute-done((f32[2,512,128]{2,1,0:T(8,128)S(1)}, f32[2,512,128]{2,1,0:T(8,128)S(1)}, u32[]{:S(2)}, u32[]{:S(2)}) %collective-permute-start.113) | collective-permute-done | bytes 524320 | tf_op jit(solution)/shard_map/ppermute | solution.py:56
  1031.3 54.9 %shard_map.77 = (f32[128,2048]{1,0:T(8,128)S(1)}, f32[256,1024]{1,0:T(8,128)S(1)}, f32[256,2048]{1,0:T(8,128)}) custom-call(s32[128]{0:T(128)S(1)} %compare_select_fusion.4.tab_ref, s32[3]{0:T(128)S(1)} %pad_add_fusion.2.info_ref, bf16[2,768,2048]{2,1,0:T(8,128)(2,1)} %pad_maximum_fusion.refs_0_, bf16[2,768,2048]{2,1,0:T(8,128)(2,1)} %collective-permute-done.91.refs_1_, ...), custom_call_target="tpu_custom_call" | custom-call | flops 34359738368 | bytes 70000000 | tf_op jit(solution)/shard_map/pallas_call | solution.py:273
  1088.4 2.3 shard_map.79
  1093.3 16.8 %collective-permute-done.108.uc_ref = f32[2,512,128]{2,1,0:T(8,128)S(1)} collective-permute-done((f32[2,512,128]{2,1,0:T(8,128)}, f32[2,512,128]{2,1,0:T(8,128)S(1)}, u32[]{:S(2)}, u32[]{:S(2)}) %collective-permute-start.108) | collective-permute-done | bytes 524320 | tf_op jit(solution)/shard_map/ppermute | solution.py:56
  1113.7 2.3 shard_map.81
  1117.3 54.7 %shard_map.84 = (f32[128,2048]{1,0:T(8,128)S(1)}, f32[256,1024]{1,0:T(8,128)S(1)}, f32[256,2048]{1,0:T(8,128)}) custom-call(s32[128]{0:T(128)S(1)} %compare_select_fusion.4.tab_ref, s32[3]{0:T(128)S(1)} %pad_add_fusion.2.info_ref, bf16[2,768,2048]{2,1,0:T(8,128)(2,1)} %pad_maximum_fusion.refs_0_, bf16[2,768,2048]{2,1,0:T(8,128)(2,1)} %collective-permute-done.91.refs_1_, ...), custom_call_target="tpu_custom_call" | custom-call | flops 34359738368 | bytes 70000000 | tf_op jit(solution)/shard_map/pallas_call | solution.py:273
  1175.0 53.7 %shard_map.83 = (f32[128,2048]{1,0:T(8,128)S(1)}, f32[256,1024]{1,0:T(8,128)S(1)}, f32[256,2048]{1,0:T(8,128)S(1)}) custom-call(s32[128]{0:T(128)S(1)} %compare_select_fusion.4.tab_ref, s32[3]{0:T(128)S(1)} %pad_add_fusion.2.info_ref, bf16[2,768,2048]{2,1,0:T(8,128)(2,1)} %pad_maximum_fusion.refs_0_, bf16[2,768,2048]{2,1,0:T(8,128)(2,1)} %collective-permute-done.91.refs_1_, ...), custom_call_target="tpu_custom_call" | custom-call | flops 34359738368 | bytes 70000000 | tf_op jit(solution)/shard_map/pallas_call | solution.py:273
  1230.8 12.8 collective-permute-done.118.uc_ref
  1243.6 32.1 %collective-permute-done.119.uy_ref = f32[2,512,128]{2,1,0:T(8,128)S(1)} collective-permute-done((f32[2,512,128]{2,1,0:T(8,128)S(1)}, f32[2,512,128]{2,1,0:T(8,128)S(1)}, u32[]{:S(2)}, u32[]{:S(2)}) %collective-permute-start.119) | collective-permute-done | bytes 524320 | tf_op jit(solution)/shard_map/ppermute | solution.py:60
  1276.0 2.3 shard_map.85
  1283.0 2.3 shard_map.87
  1285.3 38.8 %collective-permute-done.135.uc_ref = f32[2,512,128]{2,1,0:T(8,128)S(1)} collective-permute-done((f32[2,512,128]{2,1,0:T(8,128)S(1)}, f32[2,512,128]{2,1,0:T(8,128)S(1)}, u32[]{:S(2)}, u32[]{:S(2)}) %collective-permute-start.135) | collective-permute-done | bytes 524320 | tf_op jit(solution)/shard_map/ppermute | solution.py:56
  1326.6 2.2 shard_map.88
  1330.4 41.7 %collective-permute-done.131.uc_ref = f32[2,512,128]{2,1,0:T(8,128)S(1)} collective-permute-done((f32[2,512,128]{2,1,0:T(8,128)S(1)}, f32[2,512,128]{2,1,0:T(8,128)S(1)}, u32[]{:S(2)}, u32[]{:S(2)}) %collective-permute-start.131) | collective-permute-done | bytes 524320 | tf_op jit(solution)/shard_map/ppermute | solution.py:56
  1374.3 2.3 shard_map.89
  1376.6 2.3 shard_map.90
  1378.9 38.0 %collective-permute-done.127.uc_ref = f32[2,512,128]{2,1,0:T(8,128)S(1)} collective-permute-done((f32[2,512,128]{2,1,0:T(8,128)S(1)}, f32[2,512,128]{2,1,0:T(8,128)S(1)}, u32[]{:S(2)}, u32[]{:S(2)}) %collective-permute-start.127) | collective-permute-done | bytes 524320 | tf_op jit(solution)/shard_map/ppermute | solution.py:56
  1417.0 2.3 shard_map.91
  (150 shorter events, 53.5 us)
Async XLA Ops:
  45.7 30.0 %collective-permute-start.93 = (bf16[2,2432,2048]{2,1,0:T(8,128)(2,1)}, bf16[2,2432,2048]{2,1,0:T(8,128)(2,1)}, u32[]{:S(2)}, u32[]{:S(2)}) collective-permute-start(bf16[2,2432,2048]{2,1,0:T(8,128)(2,1)} %pack_rest.1.own_ref.refs_4_), channel_id=1, source_target_pairs={{0,1},{1,0},{2,3},{3,2},{4,5},{5,4},{6,7},{7,6}} | collective-permute-start | bytes 59768840 | tf_op jit(solution)/shard_map/ppermute | solution.py:44
  51.6 136.6 %collective-permute-start.92 = (bf16[2,768,2048]{2,1,0:T(8,128)(2,1)}, bf16[2,768,2048]{2,1,0:T(8,128)(2,1)}, u32[]{:S(2)}, u32[]{:S(2)}) collective-permute-start(bf16[2,768,2048]{2,1,0:T(8,128)(2,1)} %pad_maximum_fusion.refs_0_), channel_id=1, source_target_pairs={{0,4},{4,0},{1,5},{5,1},{2,6},{6,2},{3,7},{7,3}} | collective-permute-start | bytes 18874376 | tf_op jit(solution)/shard_map/ppermute | solution.py:56
  53.8 643.7 %collective-permute-start.91 = (bf16[2,768,2048]{2,1,0:T(8,128)(2,1)}, bf16[2,768,2048]{2,1,0:T(8,128)(2,1)}, u32[]{:S(2)}, u32[]{:S(2)}) collective-permute-start(bf16[2,768,2048]{2,1,0:T(8,128)(2,1)} %pad_maximum_fusion.refs_0_), channel_id=1, source_target_pairs={{0,1},{1,0},{2,3},{3,2},{4,5},{5,4},{6,7},{7,6}} | collective-permute-start | bytes 18874376 | tf_op jit(solution)/shard_map/ppermute | solution.py:44
  202.5 138.5 %collective-permute-start.50 = (bf16[2,768,2048]{2,1,0:T(8,128)(2,1)S(1)}, bf16[2,768,2048]{2,1,0:T(8,128)(2,1)}, u32[]{:S(2)}, u32[]{:S(2)}) collective-permute-start(bf16[2,768,2048]{2,1,0:T(8,128)(2,1)S(1)} %get-tuple-element.294), channel_id=1, source_target_pairs={{0,4},{4,0},{1,5},{5,1},{2,6},{6,2},{3,7},{7,3}} | collective-permute-start | bytes 18874376 | tf_op jit(solution)/shard_map/cond/branch_13_fun/ppermute | solution.py:56
  203.9 268.8 %collective-permute-start.51 = (bf16[2,768,2048]{2,1,0:T(8,128)(2,1)S(1)}, bf16[2,768,2048]{2,1,0:T(8,128)(2,1)}, u32[]{:S(2)}, u32[]{:S(2)}) collective-permute-start(bf16[2,768,2048]{2,1,0:T(8,128)(2,1)S(1)} %get-tuple-element.293), channel_id=1, source_target_pairs={{0,4},{4,0},{1,5},{5,1},{2,6},{6,2},{3,7},{7,3}} | collective-permute-start | bytes 18874376 | tf_op jit(solution)/shard_map/cond/branch_13_fun/ppermute | solution.py:56
  204.5 301.8 %collective-permute-start.49 = (bf16[2,768,2048]{2,1,0:T(8,128)(2,1)}, bf16[2,768,2048]{2,1,0:T(8,128)(2,1)}, u32[]{:S(2)}, u32[]{:S(2)}) collective-permute-start(bf16[2,768,2048]{2,1,0:T(8,128)(2,1)} %get-tuple-element.97), channel_id=1, source_target_pairs={{0,1},{1,0},{2,3},{3,2},{4,5},{5,4},{6,7},{7,6}} | collective-permute-start | bytes 18874376 | tf_op jit(solution)/shard_map/cond/branch_13_fun/ppermute | solution.py:44
  341.0 165.4 %collective-permute-start.53 = (bf16[2,768,2048]{2,1,0:T(8,128)(2,1)}, bf16[2,768,2048]{2,1,0:T(8,128)(2,1)}, u32[]{:S(2)}, u32[]{:S(2)}) collective-permute-start(bf16[2,768,2048]{2,1,0:T(8,128)(2,1)} %collective-permute-done.50), channel_id=1, source_target_pairs={{0,1},{1,0},{2,3},{3,2},{4,5},{5,4},{6,7},{7,6}} | collective-permute-start | bytes 18874376 | tf_op jit(solution)/shard_map/cond/branch_13_fun/ppermute | solution.py:44
  472.6 33.7 %collective-permute-start.54 = (bf16[2,768,2048]{2,1,0:T(8,128)(2,1)}, bf16[2,768,2048]{2,1,0:T(8,128)(2,1)}, u32[]{:S(2)}, u32[]{:S(2)}) collective-permute-start(bf16[2,768,2048]{2,1,0:T(8,128)(2,1)} %collective-permute-done.51), channel_id=1, source_target_pairs={{0,1},{1,0},{2,3},{3,2},{4,5},{5,4},{6,7},{7,6}} | collective-permute-start | bytes 18874376 | tf_op jit(solution)/shard_map/cond/branch_13_fun/ppermute | solution.py:44
  514.8 182.7 %collective-permute-start.97 = (bf16[1024,2048]{1,0:T(8,128)(2,1)}, bf16[1024,2048]{1,0:T(8,128)(2,1)}, u32[]{:S(2)}, u32[]{:S(2)}) collective-permute-start(bf16[1024,2048]{1,0:T(8,128)(2,1)} %dynamic-slice_bitcast_fusion.refs_16_), channel_id=1, source_target_pairs={{0,2},{2,0},{1,3},{3,1},{4,6},{6,4},{5,7},{7,5}} | collective-permute-start | bytes 12582920 | tf_op jit(solution)/shard_map/ppermute | solution.py:48
  523.2 130.3 %collective-permute-start.95 = (bf16[2,512,1024]{2,1,0:T(8,128)(2,1)}, bf16[2,512,1024]{2,1,0:T(8,128)(2,1)}, u32[]{:S(2)}, u32[]{:S(2)}) collective-permute-start(bf16[2,512,1024]{2,1,0:T(8,128)(2,1)} %get-tuple-element.312), channel_id=1, source_target_pairs={{0,2},{2,0},{1,3},{3,1},{4,6},{6,4},{5,7},{7,5}} | collective-permute-start | bytes 6291464 | tf_op jit(solution)/shard_map/ppermute | solution.py:48
  523.8 173.7 %collective-permute-start.96 = (bf16[2,512,1024]{2,1,0:T(8,128)(2,1)}, bf16[2,512,1024]{2,1,0:T(8,128)(2,1)}, u32[]{:S(2)}, u32[]{:S(2)}) collective-permute-start(bf16[2,512,1024]{2,1,0:T(8,128)(2,1)} %get-tuple-element.310), channel_id=1, source_target_pairs={{0,3},{3,0},{1,2},{2,1},{4,7},{7,4},{5,6},{6,5}} | collective-permute-start | bytes 6291464 | tf_op jit(solution)/shard_map/ppermute | solution.py:52
  751.1 53.7 %collective-permute-start.99 = (f32[256,2048]{1,0:T(8,128)S(1)}, f32[256,2048]{1,0:T(8,128)S(1)}, u32[]{:S(2)}, u32[]{:S(2)}) collective-permute-start(f32[256,2048]{1,0:T(8,128)S(1)} %get-tuple-element.210), channel_id=1, source_target_pairs={{0,2},{2,0},{1,3},{3,1},{4,6},{6,4},{5,7},{7,5}} | collective-permute-start | bytes 6291464 | tf_op jit(solution)/shard_map/ppermute | solution.py:48
  804.8 60.6 %collective-permute-start.98 = (f32[256,2048]{1,0:T(8,128)S(1)}, f32[256,2048]{1,0:T(8,128)S(1)}, u32[]{:S(2)}, u32[]{:S(2)}) collective-permute-start(f32[256,2048]{1,0:T(8,128)S(1)} %get-tuple-element.207), channel_id=1, source_target_pairs={{0,2},{2,0},{1,3},{3,1},{4,6},{6,4},{5,7},{7,5}} | collective-permute-start | bytes 6291464 | tf_op jit(solution)/shard_map/ppermute | solution.py:48
  808.3 174.6 %collective-permute-start.103 = (f32[2,512,128]{2,1,0:T(8,128)}, f32[2,512,128]{2,1,0:T(8,128)S(1)}, u32[]{:S(2)}, u32[]{:S(2)}) collective-permute-start(f32[2,512,128]{2,1,0:T(8,128)} %get-tuple-element.219), channel_id=1, source_target_pairs={{0,5},{1,4},{2,7},{3,6},{4,1},{5,0},{6,3},{7,2}} | collective-permute-start | bytes 1572872 | tf_op jit(solution)/shard_map/ppermute | solution.py:60
  809.7 173.8 %collective-permute-start.104 = (f32[2,512,128]{2,1,0:T(8,128)}, f32[2,512,128]{2,1,0:T(8,128)S(1)}, u32[]{:S(2)}, u32[]{:S(2)}) collective-permute-start(f32[2,512,128]{2,1,0:T(8,128)} %get-tuple-element.219), channel_id=1, source_target_pairs={{0,1},{1,0},{2,3},{3,2},{4,5},{5,4},{6,7},{7,6}} | collective-permute-start | bytes 1572872 | tf_op jit(solution)/shard_map/ppermute | solution.py:44
  810.1 174.6 %collective-permute-start.101 = (f32[128,2048]{1,0:T(8,128)}, f32[128,2048]{1,0:T(8,128)S(1)}, u32[]{:S(2)}, u32[]{:S(2)}) collective-permute-start(f32[128,2048]{1,0:T(8,128)} %get-tuple-element.217.refs_18_), channel_id=1, source_target_pairs={{0,4},{4,0},{1,5},{5,1},{2,6},{6,2},{3,7},{7,3}} | collective-permute-start | bytes 3145736 | tf_op jit(solution)/shard_map/ppermute | solution.py:56
  865.3 60.0 %collective-permute-start.105 = (f32[256,2048]{1,0:T(8,128)}, f32[256,2048]{1,0:T(8,128)S(1)}, u32[]{:S(2)}, u32[]{:S(2)}) collective-permute-start(f32[256,2048]{1,0:T(8,128)} %get-tuple-element.222), channel_id=1, source_target_pairs={{0,2},{2,0},{1,3},{3,1},{4,6},{6,4},{5,7},{7,5}} | collective-permute-start | bytes 6291464 | tf_op jit(solution)/shard_map/ppermute | solution.py:48
  865.4 117.2 %collective-permute-start.102 = (f32[2,512,128]{2,1,0:T(8,128)}, f32[2,512,128]{2,1,0:T(8,128)S(1)}, u32[]{:S(2)}, u32[]{:S(2)}) collective-permute-start(f32[2,512,128]{2,1,0:T(8,128)} %copy-done.12), channel_id=1, source_target_pairs={{0,4},{4,0},{1,5},{5,1},{2,6},{6,2},{3,7},{7,3}} | collective-permute-start | bytes 1572872 | tf_op jit(solution)/shard_map/ppermute | solution.py:56
  925.3 62.1 %collective-permute-start.100 = (f32[256,2048]{1,0:T(8,128)}, f32[256,2048]{1,0:T(8,128)S(1)}, u32[]{:S(2)}, u32[]{:S(2)}) collective-permute-start(f32[256,2048]{1,0:T(8,128)} %get-tuple-element.216), channel_id=1, source_target_pairs={{0,2},{2,0},{1,3},{3,1},{4,6},{6,4},{5,7},{7,5}} | collective-permute-start | bytes 6291464 | tf_op jit(solution)/shard_map/ppermute | solution.py:48
  982.6 104.1 %collective-permute-start.112 = (f32[128,2048]{1,0:T(8,128)}, f32[128,2048]{1,0:T(8,128)S(1)}, u32[]{:S(2)}, u32[]{:S(2)}) collective-permute-start(f32[128,2048]{1,0:T(8,128)} %get-tuple-element.213.refs_18_), channel_id=1, source_target_pairs={{0,4},{4,0},{1,5},{5,1},{2,6},{6,2},{3,7},{7,3}} | collective-permute-start | bytes 3145736 | tf_op jit(solution)/shard_map/ppermute | solution.py:56
  982.9 103.3 %collective-permute-start.114 = (f32[2,512,128]{2,1,0:T(8,128)}, f32[2,512,128]{2,1,0:T(8,128)S(1)}, u32[]{:S(2)}, u32[]{:S(2)}) collective-permute-start(f32[2,512,128]{2,1,0:T(8,128)} %get-tuple-element.240), channel_id=1, source_target_pairs={{0,5},{1,4},{2,7},{3,6},{4,1},{5,0},{6,3},{7,2}} | collective-permute-start | bytes 1572872 | tf_op jit(solution)/shard_map/ppermute | solution.py:60
  983.5 102.7 %collective-permute-start.115 = (f32[2,512,128]{2,1,0:T(8,128)}, f32[2,512,128]{2,1,0:T(8,128)S(1)}, u32[]{:S(2)}, u32[]{:S(2)}) collective-permute-start(f32[2,512,128]{2,1,0:T(8,128)} %get-tuple-element.240), channel_id=1, source_target_pairs={{0,1},{1,0},{2,3},{3,2},{4,5},{5,4},{6,7},{7,6}} | collective-permute-start | bytes 1572872 | tf_op jit(solution)/shard_map/ppermute | solution.py:44
  984.7 46.6 %collective-permute-start.113 = (f32[2,512,128]{2,1,0:T(8,128)S(1)}, f32[2,512,128]{2,1,0:T(8,128)S(1)}, u32[]{:S(2)}, u32[]{:S(2)}) collective-permute-start(f32[2,512,128]{2,1,0:T(8,128)S(1)} %copy-done.11), channel_id=1, source_target_pairs={{0,4},{4,0},{1,5},{5,1},{2,6},{6,2},{3,7},{7,3}} | collective-permute-start | bytes 1572872 | tf_op jit(solution)/shard_map/ppermute | solution.py:56
  987.4 125.2 %collective-permute-start.107 = (f32[128,2048]{1,0:T(8,128)S(1)}, f32[128,2048]{1,0:T(8,128)S(1)}, u32[]{:S(2)}, u32[]{:S(2)}) collective-permute-start(f32[128,2048]{1,0:T(8,128)S(1)} %get-tuple-element.233.refs_18_), channel_id=1, source_target_pairs={{0,4},{4,0},{1,5},{5,1},{2,6},{6,2},{3,7},{7,3}} | collective-permute-start | bytes 3145736 | tf_op jit(solution)/shard_map/ppermute | solution.py:56
  1031.3 59.4 %collective-permute-start.111 = (f32[256,2048]{1,0:T(8,128)}, f32[256,2048]{1,0:T(8,128)S(1)}, u32[]{:S(2)}, u32[]{:S(2)}) collective-permute-start(f32[256,2048]{1,0:T(8,128)} %get-tuple-element.238), channel_id=1, source_target_pairs={{0,2},{2,0},{1,3},{3,1},{4,6},{6,4},{5,7},{7,5}} | collective-permute-start | bytes 6291464 | tf_op jit(solution)/shard_map/ppermute | solution.py:48
  1086.3 26.3 %collective-permute-start.110 = (f32[2,512,128]{2,1,0:T(8,128)}, f32[2,512,128]{2,1,0:T(8,128)S(1)}, u32[]{:S(2)}, u32[]{:S(2)}) collective-permute-start(f32[2,512,128]{2,1,0:T(8,128)} %get-tuple-element.235), channel_id=1, source_target_pairs={{0,1},{1,0},{2,3},{3,2},{4,5},{5,4},{6,7},{7,6}} | collective-permute-start | bytes 1572872 | tf_op jit(solution)/shard_map/ppermute | solution.py:44
  1090.7 140.1 %collective-permute-start.122 = (f32[128,2048]{1,0:T(8,128)S(1)}, f32[128,2048]{1,0:T(8,128)S(1)}, u32[]{:S(2)}, u32[]{:S(2)}) collective-permute-start(f32[128,2048]{1,0:T(8,128)S(1)} %get-tuple-element.229.refs_18_), channel_id=1, source_target_pairs={{0,4},{4,0},{1,5},{5,1},{2,6},{6,2},{3,7},{7,3}} | collective-permute-start | bytes 3145736 | tf_op jit(solution)/shard_map/ppermute | solution.py:56
  1110.1 118.6 %collective-permute-start.124 = (f32[2,512,128]{2,1,0:T(8,128)}, f32[2,512,128]{2,1,0:T(8,128)S(1)}, u32[]{:S(2)}, u32[]{:S(2)}) collective-permute-start(f32[2,512,128]{2,1,0:T(8,128)} %get-tuple-element.260), channel_id=1, source_target_pairs={{0,5},{1,4},{2,7},{3,6},{4,1},{5,0},{6,3},{7,2}} | collective-permute-start | bytes 1572872 | tf_op jit(solution)/shard_map/ppermute | solution.py:60
  1111.8 118.0 %collective-permute-start.125 = (f32[2,512,128]{2,1,0:T(8,128)}, f32[2,512,128]{2,1,0:T(8,128)S(1)}, u32[]{:S(2)}, u32[]{:S(2)}) collective-permute-start(f32[2,512,128]{2,1,0:T(8,128)} %get-tuple-element.260), channel_id=1, source_target_pairs={{0,1},{1,0},{2,3},{3,2},{4,5},{5,4},{6,7},{7,6}} | collective-permute-start | bytes 1572872 | tf_op jit(solution)/shard_map/ppermute | solution.py:44
  1112.6 59.4 %collective-permute-start.106 = (f32[256,2048]{1,0:T(8,128)}, f32[256,2048]{1,0:T(8,128)S(1)}, u32[]{:S(2)}, u32[]{:S(2)}) collective-permute-start(f32[256,2048]{1,0:T(8,128)} %get-tuple-element.232), channel_id=1, source_target_pairs={{0,2},{2,0},{1,3},{3,1},{4,6},{6,4},{5,7},{7,5}} | collective-permute-start | bytes 6291464 | tf_op jit(solution)/shard_map/ppermute | solution.py:48
  1112.6 116.1 %collective-permute-start.123 = (f32[2,512,128]{2,1,0:T(8,128)}, f32[2,512,128]{2,1,0:T(8,128)S(1)}, u32[]{:S(2)}, u32[]{:S(2)}) collective-permute-start(f32[2,512,128]{2,1,0:T(8,128)} %get-tuple-element.259), channel_id=1, source_target_pairs={{0,4},{4,0},{1,5},{5,1},{2,6},{6,2},{3,7},{7,3}} | collective-permute-start | bytes 1572872 | tf_op jit(solution)/shard_map/ppermute | solution.py:56
  1172.0 108.2 %collective-permute-start.121 = (f32[256,2048]{1,0:T(8,128)}, f32[256,2048]{1,0:T(8,128)S(1)}, u32[]{:S(2)}, u32[]{:S(2)}) collective-permute-start(f32[256,2048]{1,0:T(8,128)} %get-tuple-element.258), channel_id=1, source_target_pairs={{0,2},{2,0},{1,3},{3,1},{4,6},{6,4},{5,7},{7,5}} | collective-permute-start | bytes 6291464 | tf_op jit(solution)/shard_map/ppermute | solution.py:48
  1228.7 97.5 %collective-permute-start.116 = (f32[256,2048]{1,0:T(8,128)S(1)}, f32[256,2048]{1,0:T(8,128)S(1)}, u32[]{:S(2)}, u32[]{:S(2)}) collective-permute-start(f32[256,2048]{1,0:T(8,128)S(1)} %get-tuple-element.252), channel_id=1, source_target_pairs={{0,2},{2,0},{1,3},{3,1},{4,6},{6,4},{5,7},{7,5}} | collective-permute-start | bytes 6291464 | tf_op jit(solution)/shard_map/ppermute | solution.py:48
  1229.7 50.5 %collective-permute-start.117 = (f32[128,2048]{1,0:T(8,128)S(1)}, f32[128,2048]{1,0:T(8,128)S(1)}, u32[]{:S(2)}, u32[]{:S(2)}) collective-permute-start(f32[128,2048]{1,0:T(8,128)S(1)} %copy-done.3), channel_id=1, source_target_pairs={{0,4},{4,0},{1,5},{5,1},{2,6},{6,2},{3,7},{7,3}} | collective-permute-start | bytes 3145736 | tf_op jit(solution)/shard_map/ppermute | solution.py:56
  1230.8 44.9 %collective-permute-start.119 = (f32[2,512,128]{2,1,0:T(8,128)S(1)}, f32[2,512,128]{2,1,0:T(8,128)S(1)}, u32[]{:S(2)}, u32[]{:S(2)}) collective-permute-start(f32[2,512,128]{2,1,0:T(8,128)S(1)} %copy-done.5), channel_id=1, source_target_pairs={{0,5},{1,4},{2,7},{3,6},{4,1},{5,0},{6,3},{7,2}} | collective-permute-start | bytes 1572872 | tf_op jit(solution)/shard_map/ppermute | solution.py:60
  1243.5 34.8 %collective-permute-start.120 = (f32[2,512,128]{2,1,0:T(8,128)S(1)}, f32[2,512,128]{2,1,0:T(8,128)S(1)}, u32[]{:S(2)}, u32[]{:S(2)}) collective-permute-start(f32[2,512,128]{2,1,0:T(8,128)S(1)} %copy-done.5), channel_id=1, source_target_pairs={{0,1},{1,0},{2,3},{3,2},{4,5},{5,4},{6,7},{7,6}} | collective-permute-start | bytes 1572872 | tf_op jit(solution)/shard_map/ppermute | solution.py:44
  1275.7 53.1 %collective-permute-start.134 = (f32[128,2048]{1,0:T(8,128)S(1)}, f32[128,2048]{1,0:T(8,128)S(1)}, u32[]{:S(2)}, u32[]{:S(2)}) collective-permute-start(f32[128,2048]{1,0:T(8,128)S(1)} %get-tuple-element.249.refs_18_), channel_id=1, source_target_pairs={{0,4},{4,0},{1,5},{5,1},{2,6},{6,2},{3,7},{7,3}} | collective-permute-start | bytes 3145736 | tf_op jit(solution)/shard_map/ppermute | solution.py:56
  1278.3 45.8 %collective-permute-start.136 = (f32[2,512,128]{2,1,0:T(8,128)S(1)}, f32[2,512,128]{2,1,0:T(8,128)S(1)}, u32[]{:S(2)}, u32[]{:S(2)}) collective-permute-start(f32[2,512,128]{2,1,0:T(8,128)S(1)} %get-tuple-element.276), channel_id=1, source_target_pairs={{0,5},{1,4},{2,7},{3,6},{4,1},{5,0},{6,3},{7,2}} | collective-permute-start | bytes 1572872 | tf_op jit(solution)/shard_map/ppermute | solution.py:60
  1280.2 44.3 %collective-permute-start.137 = (f32[2,512,128]{2,1,0:T(8,128)S(1)}, f32[2,512,128]{2,1,0:T(8,128)S(1)}, u32[]{:S(2)}, u32[]{:S(2)}) collective-permute-start(f32[2,512,128]{2,1,0:T(8,128)S(1)} %get-tuple-element.276), channel_id=1, source_target_pairs={{0,1},{1,0},{2,3},{3,2},{4,5},{5,4},{6,7},{7,6}} | collective-permute-start | bytes 1572872 | tf_op jit(solution)/shard_map/ppermute | solution.py:44
  1280.2 43.8 %collective-permute-start.135 = (f32[2,512,128]{2,1,0:T(8,128)S(1)}, f32[2,512,128]{2,1,0:T(8,128)S(1)}, u32[]{:S(2)}, u32[]{:S(2)}) collective-permute-start(f32[2,512,128]{2,1,0:T(8,128)S(1)} %copy-done.7), channel_id=1, source_target_pairs={{0,4},{4,0},{1,5},{5,1},{2,6},{6,2},{3,7},{7,3}} | collective-permute-start | bytes 1572872 | tf_op jit(solution)/shard_map/ppermute | solution.py:56
  1324.1 48.1 %collective-permute-start.132 = (f32[2,512,128]{2,1,0:T(8,128)S(1)}, f32[2,512,128]{2,1,0:T(8,128)S(1)}, u32[]{:S(2)}, u32[]{:S(2)}) collective-permute-start(f32[2,512,128]{2,1,0:T(8,128)S(1)} %get-tuple-element.274), channel_id=1, source_target_pairs={{0,5},{1,4},{2,7},{3,6},{4,1},{5,0},{6,3},{7,2}} | collective-permute-start | bytes 1572872 | tf_op jit(solution)/shard_map/ppermute | solution.py:60
  1324.2 48.6 %collective-permute-start.133 = (f32[2,512,128]{2,1,0:T(8,128)S(1)}, f32[2,512,128]{2,1,0:T(8,128)S(1)}, u32[]{:S(2)}, u32[]{:S(2)}) collective-permute-start(f32[2,512,128]{2,1,0:T(8,128)S(1)} %get-tuple-element.274), channel_id=1, source_target_pairs={{0,1},{1,0},{2,3},{3,2},{4,5},{5,4},{6,7},{7,6}} | collective-permute-start | bytes 1572872 | tf_op jit(solution)/shard_map/ppermute | solution.py:44
  1324.6 52.1 %collective-permute-start.130 = (f32[128,2048]{1,0:T(8,128)S(1)}, f32[128,2048]{1,0:T(8,128)S(1)}, u32[]{:S(2)}, u32[]{:S(2)}) collective-permute-start(f32[128,2048]{1,0:T(8,128)S(1)} %get-tuple-element.272), channel_id=1, source_target_pairs={{0,4},{4,0},{1,5},{5,1},{2,6},{6,2},{3,7},{7,3}} | collective-permute-start | bytes 3145736 | tf_op jit(solution)/shard_map/ppermute | solution.py:56
  1326.2 45.9 %collective-permute-start.131 = (f32[2,512,128]{2,1,0:T(8,128)S(1)}, f32[2,512,128]{2,1,0:T(8,128)S(1)}, u32[]{:S(2)}, u32[]{:S(2)}) collective-permute-start(f32[2,512,128]{2,1,0:T(8,128)S(1)} %get-tuple-element.273), channel_id=1, source_target_pairs={{0,4},{4,0},{1,5},{5,1},{2,6},{6,2},{3,7},{7,3}} | collective-permute-start | bytes 1572872 | tf_op jit(solution)/shard_map/ppermute | solution.py:56
  1328.8 88.2 %collective-permute-start.126 = (f32[128,2048]{1,0:T(8,128)S(1)}, f32[128,2048]{1,0:T(8,128)S(1)}, u32[]{:S(2)}, u32[]{:S(2)}) collective-permute-start(f32[128,2048]{1,0:T(8,128)S(1)} %get-tuple-element.269), channel_id=1, source_target_pairs={{0,4},{4,0},{1,5},{5,1},{2,6},{6,2},{3,7},{7,3}} | collective-permute-start | bytes 3145736 | tf_op jit(solution)/shard_map/ppermute | solution.py:56
  1372.2 44.8 %collective-permute-start.128 = (f32[2,512,128]{2,1,0:T(8,128)S(1)}, f32[2,512,128]{2,1,0:T(8,128)S(1)}, u32[]{:S(2)}, u32[]{:S(2)}) collective-permute-start(f32[2,512,128]{2,1,0:T(8,128)S(1)} %get-tuple-element.271), channel_id=1, source_target_pairs={{0,5},{1,4},{2,7},{3,6},{4,1},{5,0},{6,3},{7,2}} | collective-permute-start | bytes 1572872 | tf_op jit(solution)/shard_map/ppermute | solution.py:60
  1372.2 44.8 %collective-permute-start.129 = (f32[2,512,128]{2,1,0:T(8,128)S(1)}, f32[2,512,128]{2,1,0:T(8,128)S(1)}, u32[]{:S(2)}, u32[]{:S(2)}) collective-permute-start(f32[2,512,128]{2,1,0:T(8,128)S(1)} %get-tuple-element.271), channel_id=1, source_target_pairs={{0,1},{1,0},{2,3},{3,2},{4,5},{5,4},{6,7},{7,6}} | collective-permute-start | bytes 1572872 | tf_op jit(solution)/shard_map/ppermute | solution.py:44
  1372.8 44.2 %collective-permute-start.127 = (f32[2,512,128]{2,1,0:T(8,128)S(1)}, f32[2,512,128]{2,1,0:T(8,128)S(1)}, u32[]{:S(2)}, u32[]{:S(2)}) collective-permute-start(f32[2,512,128]{2,1,0:T(8,128)S(1)} %get-tuple-element.270), channel_id=1, source_target_pairs={{0,4},{4,0},{1,5},{5,1},{2,6},{6,2},{3,7},{7,3}} | collective-permute-start | bytes 1572872 | tf_op jit(solution)/shard_map/ppermute | solution.py:56
  (21 other events, 405.9 us)

commit v2 on v1

v2 whole, which is shorter than its diff:
```python
import jax
import jax.numpy as jnp
from jax import lax
from jax.experimental import pallas as pl
from jax.experimental.pallas import tpu as pltpu
from jax.sharding import PartitionSpec as P


D = 2048
TOK = 1024
MICRO = 3
BASE = 256
REST = TOK - BASE
TM = 128
NT = MICRO * REST // TM
RROWS = MICRO * REST + TM
FIRST = 3
CAPS = (6, 6, 3)
G = 4
M = G * TM
FB = 256
HB = FB // 2
NCH = D // FB
HALF = 1024
WH = 512
C1 = 0.7978845608028654
C3 = 0.044715
BF = jnp.bfloat16
F32 = jnp.float32


ANY = pl.BlockSpec(memory_space=pl.ANY)
SM = pl.BlockSpec(memory_space=pltpu.SMEM)
VM = pl.BlockSpec(memory_space=pltpu.VMEM)
MIB = 1024 * 1024

CORE = [(0, 1), (1, 0), (2, 3), (3, 2)]
XSWAP = [(0, 2), (2, 0), (1, 3), (3, 1)]
XDIAG = [(0, 3), (3, 0), (1, 2), (2, 1)]
YSWAP = [(0, 1), (1, 0)]
YDIAG = [(r * 4 + f, (1 - r) * 4 + (f ^ 1)) for r in range(2) for f in range(4)]


def core_swap(v):
    return lax.ppermute(v, "fsdp", CORE)


def x_swap(v):
    return lax.ppermute(v, "fsdp", XSWAP)


def x_diag(v):
    return lax.ppermute(v, "fsdp", XDIAG)


def y_swap(v):
    return lax.ppermute(v, "replica", YSWAP)


def y_diag(v):
    return lax.ppermute(v, ("replica", "fsdp"), YDIAG)


def cost(flops, nbytes):
    return pl.CostEstimate(flops=flops, bytes_accessed=nbytes, transcendentals=0)


def pack_rest(x_in, dy, rest, offs):
    def kern(rest_ref, offs_ref, x_ref, d_ref, out_ref, buf, zero, isem, osem, zsem):
        loads = []
        for k in range(MICRO):
            for a, ref in enumerate((x_ref, d_ref)):
                cp = pltpu.make_async_copy(ref.at[k, pl.ds(BASE, REST), :], buf.at[k, a], isem.at[k, a])
                cp.start()
                loads.append(cp)
        zero[...] = jnp.zeros_like(zero)
        for k in range(MICRO):
            n = rest_ref[k]
            for a in range(2):
                loads[2 * k + a].wait()
                for r in range(0, REST, TM):
                    row = lax.broadcasted_iota(jnp.int32, (TM, D), 0) + r
                    blk = buf[k, a, r : r + TM, :]
                    buf[k, a, r : r + TM, :] = jnp.where(row < n, blk, jnp.zeros_like(blk))
            o = pl.multiple_of(offs_ref[k], 16)
            cps = [
                pltpu.make_async_copy(buf.at[k, a], out_ref.at[a, pl.ds(o, REST), :], osem.at[a]) for a in range(2)
            ]
            for cp in cps:
                cp.start()
            for cp in cps:
                cp.wait()
        for o in (pl.multiple_of(offs_ref[MICRO], 16), MICRO * REST):
            cps = [pltpu.make_async_copy(zero, out_ref.at[a, pl.ds(o, TM), :], zsem.at[a]) for a in range(2)]
            for cp in cps:
                cp.start()
            for cp in cps:
                cp.wait()

    return pl.pallas_call(
        kern,
        in_specs=[SM, SM, ANY, ANY],
        out_specs=ANY,
        out_shape=jax.ShapeDtypeStruct((2, RROWS, D), BF),
        scratch_shapes=[
            pltpu.VMEM((MICRO, 2, REST, D), BF),
            pltpu.VMEM((TM, D), BF),
            pltpu.SemaphoreType.DMA((MICRO, 2)),
            pltpu.SemaphoreType.DMA((2,)),
            pltpu.SemaphoreType.DMA((2,)),
        ],
        compiler_params=pltpu.CompilerParams(vmem_limit_bytes=40 * MIB),
        cost_estimate=cost(15_000_000_000, 50_000_000),
        name="pack_rest",
    )(rest, offs, x_in, dy)


def build_send(own, sib, info):
    def kern(info_ref, own_ref, sib_ref, *refs):
        outs, (buf, isem, osem) = refs[:4], refs[4:]
        n, mine, shift = info_ref[0], info_ref[1], info_ref[2]
        starts = (0, FIRST, info_ref[3], info_ref[4])

        def load(i, slot):
            @pl.when(i < mine)
            def _():
                r = pl.multiple_of(i * TM, TM)
                pltpu.make_async_copy(own_ref.at[:, pl.ds(r, TM), :], buf.at[slot], isem.at[slot]).start()

            @pl.when(i >= mine)
            def _():
                r = pl.multiple_of((i + shift) * TM, TM)
                pltpu.make_async_copy(sib_ref.at[:, pl.ds(r, TM), :], buf.at[slot], isem.at[slot]).start()

        def store(i, slot):
            for k in range(4):
                here = i >= starts[k]
                if k < 3:
                    here = jnp.logical_and(here, i < starts[k + 1])

                @pl.when(here)
                def _():
                    r = pl.multiple_of((i - starts[k]) * TM, TM)
                    pltpu.make_async_copy(buf.at[slot], outs[k].at[:, pl.ds(r, TM), :], osem.at[slot]).start()

        def stored(slot):
            pltpu.make_async_copy(buf.at[slot], outs[0].at[:, pl.ds(0, TM), :], osem.at[slot]).wait()

        for s in range(3):

            @pl.when(s < n)
            def _():
                load(s, s)

        def body(i, _):
            slot = lax.rem(i, 4)
            pltpu.make_async_copy(own_ref.at[:, pl.ds(0, TM), :], buf.at[slot], isem.at[slot]).wait()
            store(i, slot)

            @pl.when(i >= 1)
            def _():
                stored(lax.rem(i + 3, 4))

            @pl.when(i + 3 < n)
            def _():
                load(i + 3, lax.rem(i + 3, 4))

            return 0

        lax.fori_loop(0, n, body, 0)

        @pl.when(n > 0)
        def _():
            stored(lax.rem(n + 3, 4))

    return pl.pallas_call(
        kern,
        in_specs=[SM, ANY, ANY],
        out_specs=[ANY] * 4,
        out_shape=[jax.ShapeDtypeStruct((2, k * TM, D), BF) for k in (FIRST, *CAPS)],
        scratch_shapes=[pltpu.VMEM((4, 2, TM, D), BF), pltpu.SemaphoreType.DMA((4,)), pltpu.SemaphoreType.DMA((4,))],
        cost_estimate=cost(10_000_000_000, 36_000_000),
        name="build_send",
    )(info, own, sib)


def gelu_and_slope(u):
    u2 = u * u
    t = jnp.tanh(u * (C1 + (C1 * C3) * u2))
    half = 0.5 + 0.5 * t
    act = u * half
    slope = half + (0.5 * u) * (1.0 - t * t) * (C1 + (3 * C1 * C3) * u2)
    return act, slope


def pick(e, lo, hi, fn):
    if hi - lo == 1:
        fn(lo)
        return
    mid = (lo + hi) // 2

    @pl.when(e < mid * 32)
    def _():
        pick(e, lo, mid, fn)

    @pl.when(e >= mid * 32)
    def _():
        pick(e, mid, hi, fn)


def issue_group(tab_ref, g, slot, src, xb, db, sem):
    for s in range(G):
        e = tab_ref[g * G + s]
        r = pl.multiple_of(lax.rem(e, 32) * TM, TM)

        def fetch(k):
            rows = pl.ds(s * TM, TM)
            pltpu.make_async_copy(src[k].at[0, pl.ds(r, TM), :], xb.at[slot, rows, :], sem.at[slot, 0]).start()
            pltpu.make_async_copy(src[k].at[1, pl.ds(r, TM), :], db.at[slot, rows, :], sem.at[slot, 1]).start()

        pick(e, 0, len(src), fetch)


def wait_group(slot, xb, db, sem):
    pltpu.make_async_copy(xb.at[slot], xb.at[slot], sem.at[slot, 0]).wait()
    pltpu.make_async_copy(db.at[slot], db.at[slot], sem.at[slot, 1]).wait()


def add_group(x, dy, wu, wd, gd, gu):
    u = jnp.dot(x, wu[...], preferred_element_type=F32).astype(BF).astype(F32)
    da = lax.dot_general(dy, wd[...], (((1,), (1,)), ((), ())), preferred_element_type=F32)
    act, slope = gelu_and_slope(u)
    dh = (da * slope).astype(BF)
    gd[...] += lax.dot_general(act.astype(BF), dy, (((0,), (0,)), ((), ())), preferred_element_type=F32)
    gu[...] += lax.dot_general(dh, x, (((0,), (0,)), ((), ())), preferred_element_type=F32)


def weight_copies(c, f, w, wub, wdb, sem):
    own, sib, fx, fd, wd_own, wd_oth = w
    cps = []
    c0 = c * HB
    co = (c % (WH // HB)) * HB
    if not isinstance(c, int):
        c0, co = pl.multiple_of(c0, HB), pl.multiple_of(co, HB)
    for a in range(2):
        for k, (ref, col) in enumerate(((own, c0), (sib, c0), (fx, co), (fd, co))):
            rows = pl.ds(pl.multiple_of((f ^ k) * 512, 512), 512)
            cps.append(
                pltpu.make_async_copy(
                    ref.at[a, :, pl.ds(col, HB)], wub.at[rows, pl.ds(a * HB, HB)], sem.at[k, a]
                )
            )
    cps.append(pltpu.make_async_copy(wd_own.at[pl.ds(c0, HB), :], wdb.at[pl.ds(0, HB), :], sem.at[4, 0]))
    cps.append(pltpu.make_async_copy(wd_oth.at[pl.ds(co, HB), :], wdb.at[pl.ds(HB, HB), :], sem.at[4, 1]))
    return cps


def gather_scratch(n_acc):
    return [
        pltpu.VMEM((2, M, D), BF),
        pltpu.VMEM((2, M, D), BF),
        pltpu.VMEM((n_acc, D, FB), BF),
        pltpu.VMEM((n_acc, FB, D), BF),
        pltpu.VMEM((n_acc, FB, D), F32),
        pltpu.VMEM((n_acc, FB, D), F32),
        pltpu.SemaphoreType.DMA((2, 2)),
        pltpu.SemaphoreType.DMA((n_acc, 5, 2)),
    ]


def early_grads(tab, info, srcs, wsets, lo_chunk, n_chunks, prior, flops):
    ns, nw, npr = len(srcs), len(wsets), len(prior)
    per = WH // HB

    def kern(tab_ref, info_ref, *refs):
        src, refs = refs[:ns], refs[ns:]
        wset = [refs[6 * k : 6 * k + 6] for k in range(nw)]
        refs = refs[6 * nw :]
        pri, refs = refs[: 2 * npr], refs[2 * npr :]
        out_d, out_u, xb, db, wub, wdb, gd, gu, sem, wsem, asem = refs
        f = info_ref[3]
        done_before = sum(p[0].shape[0] for p in prior)

        def lo(q):
            return jnp.where(q < done_before, info_ref[0], 0)

        hi = info_ref[1]

        def weights(q, slot, act):
            c = lo_chunk + q
            for k in range(nw):
                here = c // per == (lo_chunk // per) + k

                @pl.when(here)
                def _():
                    for cp in weight_copies(c, f, wset[k], wub.at[slot], wdb.at[slot], wsem.at[slot]):
                        act(cp)

        def start(cp):
            cp.start()

        def wait(cp):
            cp.wait()

        def results(q, slot):
            return (
                pltpu.make_async_copy(gd.at[slot], out_d.at[q], asem.at[slot, 0]),
                pltpu.make_async_copy(gu.at[slot], out_u.at[q], asem.at[slot, 1]),
            )

        issue_group(tab_ref, lo(0), 0, src, xb, db, sem)
        weights(0, 0, start)

        def chunk(q, t):
            ws = lax.rem(q, 2)

            @pl.when(q + 1 < n_chunks)
            def _():
                weights(q + 1, 1 - ws, start)

            @pl.when(q >= 2)
            def _():
                for cp in results(q - 2, ws):
                    cp.wait()

            base = 0
            for k in range(npr):
                size = prior[k][0].shape[0]
                lo_q, hi_q = base, base + size
                base = hi_q

                @pl.when(jnp.logical_and(q >= lo_q, q < hi_q))
                def _():
                    cps = (
                        pltpu.make_async_copy(pri[2 * k].at[q - lo_q], gd.at[ws], asem.at[ws, 0]),
                        pltpu.make_async_copy(pri[2 * k + 1].at[q - lo_q], gu.at[ws], asem.at[ws, 1]),
                    )
                    for cp in cps:
                        cp.start()
                    for cp in cps:
                        cp.wait()

            @pl.when(q >= base)
            def _():
                gd[ws] = jnp.zeros((FB, D), F32)
                gu[ws] = jnp.zeros((FB, D), F32)

            weights(q, ws, wait)

            def group(g, t):
                slot = lax.rem(t, 2)
                last = g + 1 == hi
                nxt = jnp.where(last, lo(q + 1), g + 1)

                @pl.when(jnp.logical_or(jnp.logical_not(last), q + 1 < n_chunks))
                def _():
                    issue_group(tab_ref, nxt, 1 - slot, src, xb, db, sem)

                wait_group(slot, xb, db, sem)
                add_group(xb[slot], db[slot], wub.at[ws], wdb.at[ws], gd.at[ws], gu.at[ws])
                return t + 1

            t = lax.fori_loop(lo(q), hi, group, t)
            for cp in results(q, ws):
                cp.start()
            return t

        lax.fori_loop(0, n_chunks, chunk, 0)
        for q in range(max(n_chunks - 2, 0), n_chunks):
            for cp in results(q, q % 2):
                cp.wait()

    flat = [w for ws in wsets for w in ws]
    pri = [a for p in prior for a in p]
    return pl.pallas_call(
        kern,
        in_specs=[SM, SM] + [ANY] * (ns + len(flat) + len(pri)),
        out_specs=[ANY] * 2,
        out_shape=[jax.ShapeDtypeStruct((n_chunks, FB, D), F32)] * 2,
        scratch_shapes=gather_scratch(2) + [pltpu.SemaphoreType.DMA((2, 2))],
        compiler_params=pltpu.CompilerParams(vmem_limit_bytes=48 * MIB),
        cost_estimate=cost(flops, 200_000_000),
    )(tab, info, *srcs, *flat, *pri)


def chunk_grads(j, tab, info, srcs, w, prior, deps):
    ns = len(srcs)

    def kern(tab_ref, info_ref, *refs):
        src, refs = refs[:ns], refs[ns:]
        wrefs, (pd, pu), refs = refs[:6], refs[6:8], refs[8 + len(deps) :]
        keep_d, keep_u, send_d, send_u, xb, db, wub, wdb, gd, gu, sem, wsem, osem = refs
        groups, xi, f = info_ref[0], info_ref[1], info_ref[2]
        wub, wdb, gd, gu = wub.at[0], wdb.at[0], gd.at[0], gu.at[0]
        cps = weight_copies(j, f, wrefs, wub, wdb, wsem.at[0])
        cps.append(pltpu.make_async_copy(pd.at[j], gd, osem.at[0]))
        cps.append(pltpu.make_async_copy(pu.at[j], gu, osem.at[1]))
        for cp in cps:
            cp.start()

        @pl.when(groups > 0)
        def _():
            issue_group(tab_ref, 0, 0, src, xb, db, sem)

        for cp in cps:
            cp.wait()

        def body(g, _):
            slot = lax.rem(g, 2)

            @pl.when(g + 1 < groups)
            def _():
                issue_group(tab_ref, g + 1, 1 - slot, src, xb, db, sem)

            wait_group(slot, xb, db, sem)
            add_group(xb[slot], db[slot], wub, wdb, gd, gu)
            return 0

        lax.fori_loop(0, groups, body, 0)
        kc = pl.multiple_of(xi * HALF, HALF)
        sc = pl.multiple_of((1 - xi) * HALF, HALF)
        ocp = [
            (gd.at[pl.ds(HB, HB), :], send_d),
            (gu.at[pl.ds(0, HB), pl.ds(sc, HALF)], send_u.at[:, pl.ds(0, HALF)]),
            (gu.at[pl.ds(HB, HB), pl.ds(sc, HALF)], send_u.at[:, pl.ds(HALF, HALF)]),
            (gd.at[pl.ds(0, HB), :], keep_d),
            (gu.at[:, pl.ds(kc, HALF)], keep_u),
        ]
        ocp = [pltpu.make_async_copy(a, b, osem.at[i]) for i, (a, b) in enumerate(ocp)]
        for cp in ocp:
            cp.start()
        for cp in ocp:
            cp.wait()

    n_in = ns + 8 + len(deps)
    return pl.pallas_call(
        kern,
        in_specs=[SM, SM] + [ANY] * n_in,
        out_specs=[ANY] * 4,
        out_shape=[
            jax.ShapeDtypeStruct((HB, D), F32),
            jax.ShapeDtypeStruct((FB, HALF), F32),
            jax.ShapeDtypeStruct((HB, D), F32),
            jax.ShapeDtypeStruct((HB, D), F32),
        ],
        scratch_shapes=gather_scratch(1) + [pltpu.SemaphoreType.DMA((5,))],
        compiler_params=pltpu.CompilerParams(vmem_limit_bytes=40 * MIB),
        cost_estimate=cost(8 * 3072 * D * FB, 40_000_000),
    )(tab, info, *srcs, *w, *prior, *deps)


def finish_down(j, pos, keep, recv, out):
    first = out is None

    def kern(pos_ref, kd, rc, *refs):
        out_d, fd, vd, sem = refs if first else refs[1:]
        y = pos_ref[0]
        vd[...] = kd[...] + rc[...]
        row = pl.multiple_of(y * HALF + j * HB, HB)
        cps = [
            pltpu.make_async_copy(vd, fd, sem.at[0]),
            pltpu.make_async_copy(vd, out_d.at[pl.ds(row, HB), :], sem.at[1]),
        ]
        for cp in cps:
            cp.start()
        for cp in cps:
            cp.wait()

    extra = [] if first else [out]
    return pl.pallas_call(
        kern,
        in_specs=[SM, VM, VM] + [ANY] * len(extra),
        out_specs=[ANY] * 2,
        out_shape=[jax.ShapeDtypeStruct((D, D), F32), jax.ShapeDtypeStruct((HB, D), F32)],
        scratch_shapes=[pltpu.VMEM((HB, D), F32), pltpu.SemaphoreType.DMA((2,))],
        input_output_aliases={} if first else {3: 0},
        compiler_params=pltpu.CompilerParams(vmem_limit_bytes=16 * MIB),
        cost_estimate=cost(2_000_000_000, 4_000_000),
    )(pos, keep, recv, *extra)


def finish_up(j, pos, keep, recv, out):
    first = out is None

    def kern(pos_ref, ku, rc, *refs):
        out_u, fuc, fus, vu, sem = refs if first else refs[1:]
        y, xi, c = pos_ref[0], pos_ref[1], pos_ref[2]
        mine = pl.ds(pl.multiple_of(c * 512, 512), 512)
        other = pl.ds(pl.multiple_of((1 - c) * 512, 512), 512)
        vu[0] = (ku[0:HB, :] + rc[:, HALF:D]).T
        vu[1] = (ku[HB:FB, :] + rc[:, 0:HALF]).T
        cps = [
            pltpu.make_async_copy(vu.at[:, other, :], fus, sem.at[0]),
            pltpu.make_async_copy(vu.at[:, mine, :], fuc, sem.at[1]),
        ]
        for a in range(2):
            xa = xi if a == 0 else 1 - xi
            col = pl.multiple_of(((2 * xa + c) * 2 + y) * HALF + j * HB, HB)
            cps.append(pltpu.make_async_copy(vu.at[a, mine, :], out_u.at[:, pl.ds(col, HB)], sem.at[2 + a]))
        for cp in cps:
            cp.start()
        for cp in cps:
            cp.wait()

    extra = [] if first else [out]
    return pl.pallas_call(
        kern,
        in_specs=[SM, VM, VM] + [ANY] * len(extra),
        out_specs=[ANY] * 3,
        out_shape=[
            jax.ShapeDtypeStruct((512, 4 * D), F32),
            jax.ShapeDtypeStruct((2, 512, HB), F32),
            jax.ShapeDtypeStruct((2, 512, HB), F32),
        ],
        scratch_shapes=[pltpu.VMEM((2, HALF, HB), F32), pltpu.SemaphoreType.DMA((4,))],
        input_output_aliases={} if first else {3: 0},
        compiler_params=pltpu.CompilerParams(vmem_limit_bytes=16 * MIB),
        cost_estimate=cost(2_000_000_000, 4_000_000),
    )(pos, keep, recv, *extra)


def store(j, pos, rd, ruc, ruy, rus, outs):
    def kern(pos_ref, d_ref, uc_ref, uy_ref, us_ref, _d, _u, out_d, out_u, vd, vu, isem, osem):
        y, xi, c = pos_ref[0], pos_ref[1], pos_ref[2]
        loads = [pltpu.make_async_copy(d_ref, vd, isem.at[0])]
        for k, r in enumerate((uc_ref, uy_ref, us_ref)):
            loads.append(pltpu.make_async_copy(r, vu.at[k], isem.at[1 + k]))
        for cp in loads:
            cp.start()
        row = pl.multiple_of((1 - y) * HALF + j * HB, HB)
        loads[0].wait()
        outc = [pltpu.make_async_copy(vd, out_d.at[pl.ds(row, HB), :], osem.at[0])]
        outc[0].start()
        for k, (cc, yy) in enumerate(((c, 1 - y), (1 - c, 1 - y), (1 - c, y))):
            loads[1 + k].wait()
            for a in range(2):
                xa = xi if a == 0 else 1 - xi
                col = pl.multiple_of(((2 * xa + cc) * 2 + yy) * HALF + j * HB, HB)
                cp = pltpu.make_async_copy(vu.at[k, a], out_u.at[:, pl.ds(col, HB)], osem.at[1 + 2 * k + a])
                cp.start()
                outc.append(cp)
        for cp in outc:
            cp.wait()

    return pl.pallas_call(
        kern,
        in_specs=[SM] + [ANY] * 6,
        out_specs=[ANY] * 2,
        out_shape=[jax.ShapeDtypeStruct((D, D), F32), jax.ShapeDtypeStruct((512, 4 * D), F32)],
        scratch_shapes=[
            pltpu.VMEM((HB, D), F32),
            pltpu.VMEM((3, 2, 512, HB), F32),
            pltpu.SemaphoreType.DMA((4,)),
            pltpu.SemaphoreType.DMA((7,)),
        ],
        input_output_aliases={5: 0, 6: 1},
        compiler_params=pltpu.CompilerParams(vmem_limit_bytes=16 * MIB),
        cost_estimate=cost(3_000_000_000, 5_000_000),
    )(pos, rd, ruc, ruy, rus, *outs)


def exchange_branch(n):
    last = min(n, CAPS[2])
    full = CAPS[1] if n - last > CAPS[0] else 0
    part = n - last - full

    def swapped(piece, k, cap):
        if k == 0:
            return jnp.zeros((2, cap * TM, D), BF)
        return y_swap(piece if k == cap else piece[:, : k * TM])

    def padded(v, cap):
        short = cap * TM - v.shape[1]
        return lax.pad(v, jnp.zeros((), BF), ((0, 0, 0), (0, short, 0), (0, 0, 0))) if short else v

    def run(p0, p1, p2, early):
        g1 = swapped(p1, full, CAPS[1])
        g0 = swapped(p0, part, CAPS[0])
        g2 = swapped(p2, last, CAPS[2])
        acc = early()
        s1 = core_swap(g1) if full else g1
        s0 = core_swap(g0) if part else g0
        return (padded(g0, CAPS[0]), g1, padded(g2, CAPS[2]), padded(s0, CAPS[0]), s1, *acc)

    return run


def solution(mesh):
    tok_spec = P(None, ("model", "replica", "fsdp"), None)
    len_spec = P(None, ("model", "replica", "fsdp"))
    w_spec = P(None, ("model", "fsdp"), None)

    def group_grads(x_in, dy, lengths, w_up, w_down):
        y, f = lax.axis_index("replica"), lax.axis_index("fsdp")
        xi, c = f // 2, f % 2
        w_up, w_down = w_up[0], w_down[0]

        lens = lax.all_gather(lengths[:, 0], ("replica", "fsdp")).astype(jnp.int32)

        s1 = jnp.stack([x_in[:, :BASE], dy[:, :BASE]]).reshape(2, MICRO * BASE, D)

        def cols(xd, cd, lo=0, n=HALF):
            own = lax.dynamic_slice(w_up, (0, ((2 * xd + cd) * 2 + y) * HALF + lo), (512, n))
            oth = lax.dynamic_slice(w_up, (0, ((2 * (1 - xd) + cd) * 2 + y) * HALF + lo), (512, n))
            return jnp.stack([own, oth])

        wd_own = lax.dynamic_slice(w_down, (y * HALF, 0), (HALF, D))
        to_x = [cols(1 - xi, c, lo, WH) for lo in (0, WH)]
        to_d = [cols(1 - xi, 1 - c, lo, WH) for lo in (0, WH)]
        wd_h = [wd_own[lo : lo + WH] for lo in (0, WH)]
        (lens, s1, to_x, to_d, wd_h) = lax.optimization_barrier((lens, s1, to_x, to_d, wd_h))
        s1_y = y_swap(s1)
        wx = []
        for h in range(2):
            a = x_swap(to_x[h])
            b = x_diag(to_d[h])
            d = x_swap(wd_h[h])
            wx.append((a, b, d))
        from_s = core_swap(cols(xi, 1 - c))
        mine = cols(xi, c)
        wsets = [(mine, from_s, a, b, wd_own, d) for a, b, d in wx]

        rest = lens - BASE
        r16 = (rest + 15) // 16 * 16
        tiles = (jnp.sum(r16, axis=1) + TM - 1) // TM
        me = y * 4 + f
        my_rest = lax.dynamic_index_in_dim(rest, me, keepdims=False)
        my16 = lax.dynamic_index_in_dim(r16, me, keepdims=False)
        offs = jnp.concatenate([jnp.zeros((1,), jnp.int32), jnp.cumsum(my16)])
        both = tiles[0::2] + tiles[1::2]
        share = jnp.stack([(both + 1) // 2, both // 2], axis=1).reshape(8)
        more = jnp.maximum(jnp.max(share) - FIRST, 0)

        def at(v, i):
            return lax.dynamic_index_in_dim(v, i, keepdims=False)

        t_own, t_sib = at(tiles, me), at(tiles, me ^ 1)
        h_own = at(share, me)
        h_y, h_ys = at(share, me ^ 4), at(share, me ^ 5)
        left = jnp.maximum(more - CAPS[2], 0)
        full = jnp.where(left > CAPS[0], CAPS[1], 0)
        at1 = FIRST + left - full
        at2 = at1 + full

        packed = pack_rest(x_in, dy, my_rest, offs)
        packed_s = core_swap(packed)
        s1_s = core_swap(s1)
        pa, p0, p1, p2 = build_send(
            packed, packed_s, jnp.stack([h_own, t_own, t_sib - h_own, at1, at2]).astype(jnp.int32)
        )
        qa = y_swap(pa)

        i = jnp.arange(64)
        n_own = 12 + t_own + t_sib
        g_own = (n_own + G - 1) // G
        k = i - g_own * G
        tab = jnp.where(i < n_own, 3 * 32 + i - 12 - t_own, 2 * 32 + NT)
        tab = jnp.where(i < 12 + t_own, 2 * 32 + i - 12, tab)
        tab = jnp.where(i < 12, (i // 6) * 32 + i % 6, tab)
        tab = jnp.where((k >= 0) & (k < 12), (4 + k // 6) * 32 + k % 6, tab).astype(jnp.int32)
        info_own = jnp.stack([0, g_own, xi, f]).astype(jnp.int32)
        info_all = jnp.stack([g_own, g_own + 3, xi, f]).astype(jnp.int32)

        i = jnp.arange(40)
        own_list = i < h_y
        t = jnp.where(own_list, i, i - h_y)
        s = jnp.where(t < FIRST, t, jnp.where(t < at1, 32 + t - FIRST, jnp.where(t < at2, 64 + t - at1, 96 + t - at2)))
        late = jnp.where(own_list, s, s + 128)
        late = jnp.where(i < h_y + h_ys, late, 256 + NT).astype(jnp.int32)
        info_late = jnp.stack([(h_y + h_ys + G - 1) // G, xi, f]).astype(jnp.int32)
        pos = jnp.stack([y, xi, c]).astype(jnp.int32)

        own_srcs = (s1, s1_s, packed, packed_s)
        acc0 = early_grads(tab, info_own, own_srcs, wsets[:1], 0, 2, [], 8 * 4096 * D * FB * 2)
        s1_ys = core_swap(s1_y)
        acc1 = early_grads(tab, info_own, own_srcs, wsets[:1], 2, 2, [], 8 * 4096 * D * FB * 2)

        def branch(n):
            run = exchange_branch(n)

            def go(p0, p1, p2, tab, info, srcs, wsets, acc0, acc1):
                return run(
                    p0, p1, p2,
                    lambda: early_grads(tab, info, srcs, wsets, 0, NCH, [acc0, acc1], 8 * 4096 * D * FB * 5),
                )

            return go

        srcs = (*own_srcs, s1_y, s1_ys)
        q0, q1, q2, q0s, q1s, accd, accu = lax.switch(
            more, [branch(n) for n in range(NT - FIRST + 1)],
            p0, p1, p2, tab, info_all, srcs, [list(w) for w in wsets], list(acc0), list(acc1),
        )
        qas = core_swap(qa)
        q2s = core_swap(q2)
        srcs = (qa, q0, q1, q2, qas, q0s, q1s, q2s, packed)

        out_d = out_u = None
        fin = []
        for j in range(NCH):
            deps = (fin[j - 2][0],) if j >= 2 else ()
            keep_d, keep_u, send_d, send_u = chunk_grads(
                j, late, info_late, srcs, wsets[j * HB // WH], (accd, accu), deps
            )
            recv_d = x_swap(send_d)
            recv_u = x_swap(send_u)
            out_d, fd = finish_down(j, pos, keep_d, recv_d, out_d)
            out_u, fuc, fus = finish_up(j, pos, keep_u, recv_u, out_u)
            rd = y_swap(fd)
            ruc = y_swap(fuc)
            ruy = y_diag(fus)
            rus = core_swap(fus)
            fin.append((fuc, (rd, ruc, ruy, rus)))
            if j >= 2:
                out_d, out_u = store(j - 2, pos, *fin[j - 2][1], (out_d, out_u))
        for j in range(NCH - 2, NCH):
            out_d, out_u = store(j, pos, *fin[j][1], (out_d, out_u))
        return out_u[None], out_d[None]

    return jax.shard_map(
        group_grads,
        mesh=mesh,
        in_specs=(tok_spec, tok_spec, len_spec, w_spec, w_spec),
        out_specs=(w_spec, w_spec),
        check_vma=False,
    )
```

time: 1430 us -> 1250 us (0.87)
  waiting for transfers between devices: 797 us -> 448 us
  starting transfers between devices: 34 us -> 129 us
  Pallas kernels: 495 us -> 551 us
    ppermute x20 -> x21, waiting for transfers between devices: 584 us -> 282 us  [y_swap(): return lax.ppermute(v, 'replica', YSWAP)]
    pallas_call x9 -> x20, Pallas kernels: 27.9 us -> 316 us  [the longest x3 277 us: early_grads(): pl.pallas_call(kern, in_specs=[SM, SM] + [ANY] * (ns + len(flat) + len(pr...]
    pallas_call x8, Pallas kernels: 435 us -> 201 us  [chunk_grads(): pl.pallas_call(kern, in_specs=[SM, SM] + [ANY] * n_in, out_specs=[ANY] *...]
    ppermute x10 -> x20, waiting for transfers between devices: 126 us -> 56.1 us  [x_swap(): return lax.ppermute(v, 'fsdp', XSWAP)]
    ppermute x20 -> x21, starting transfers between devices: 20.8 us -> 76.3 us  [y_swap(): return lax.ppermute(v, 'replica', YSWAP)]
    ppermute x8, starting transfers between devices: 5.7 us -> 32 us  [y_diag(): return lax.ppermute(v, ('replica', 'fsdp'), YDIAG)]
    ppermute x8, waiting for transfers between devices: 32.2 us -> 57.4 us  [y_diag(): return lax.ppermute(v, ('replica', 'fsdp'), YDIAG)]
    ppermute x1 -> x2, waiting for transfers between devices: 44 us -> 44.7 us  [x_diag(): return lax.ppermute(v, 'fsdp', XDIAG)]
  transfers between devices with their start and end apart: 54 -> 67, of which waited for: 14 -> 20; matrix products, arithmetic and copies ran while one was open for 2% -> 2% of each run, Pallas kernels for 30% -> 41%
where the time goes in v2:
time: 1250 us; the launch traced here: 1240 us
  Pallas kernels  551 us (44%)
  waiting for transfers between devices  448 us (36%)
  starting transfers between devices  129 us (10%)
  local copies, waits for them, and re-layouts  42 us (3%)
  loops' own time  29.2 us (2%)
  blocking collectives  25 us (2%)
  other arithmetic  13.8 us (1%)
    ppermute x21, waiting for transfers between devices, y_swap(): return lax.ppermute(v, 'replica', YSWAP)  282 us
    pallas_call x3, Pallas kernels, early_grads(): pl.pallas_call(kern, in_specs=[SM, SM] + [ANY] * (ns + len(flat) + len(pr...  277 us
    pallas_call x8, Pallas kernels, chunk_grads(): pl.pallas_call(kern, in_specs=[SM, SM] + [ANY] * n_in, out_specs=[ANY] *...  201 us
    ppermute x21, starting transfers between devices, y_swap(): return lax.ppermute(v, 'replica', YSWAP)  76.3 us
    ppermute x8, waiting for transfers between devices, y_diag(): return lax.ppermute(v, ('replica', 'fsdp'), YDIAG)  57.4 us
    ppermute x20, waiting for transfers between devices, x_swap(): return lax.ppermute(v, 'fsdp', XSWAP)  56.1 us
    ppermute x2, waiting for transfers between devices, x_diag(): return lax.ppermute(v, 'fsdp', XDIAG)  44.7 us
    ppermute x8, starting transfers between devices, y_diag(): return lax.ppermute(v, ('replica', 'fsdp'), YDIAG)  32 us
  transfers between devices with their start and end apart: 67, of which 20 were waited for; matrix products, arithmetic and copies ran while one was open for 2% of the time, Pallas kernels for 41%

profile of v2, /device:TPU:0, one launch (start us, length us, event | category | flops | bytes accessed | tf_op | source)
XLA Modules:
  0.0 1244.5 jit_solution(8131570571321036479)
XLA Ops:
  1.5 25.0 %all-reduce.22 = s32[24]{0:T(128)S(1)} all-reduce(s32[24]{0:T(128)S(1)} %bitcast_dynamic-update-slice_fusion), channel_id=2, replica_groups=mesh['model'=1,'replica'=2,'fsdp'=4] {'replica','fsdp'}, use_global_device_ids=true, to_apply=%add.22 | all-reduce | flops 24 | bytes 192
  26.5 4.1 slice.61
  30.7 5.2 pad_maximum_fusion.refs_0_
  35.9 4.8 dynamic-slice_bitcast_fusion.1
  46.2 4.6 copy-done
  50.7 14.0 %pack_rest.1.own_ref.refs_2_.refs_8_ = bf16[2,2432,2048]{2,1,0:T(8,128)(2,1)} custom-call(s32[3]{0:T(128)S(1)} %fusion.8.rest_ref, s32[4]{0:T(128)S(1)} %pad_add_fusion.2.offs_ref, bf16[3,1024,2048]{2,1,0:T(8,128)(2,1)S(1)} %copy-done, bf16[3,1024,2048]{2,1,0:T(8,128)(2,1)} %d_ref.1), custom_call_target="tpu_custom_call" | custom-call | flops 15000000512 | bytes 50000000 | tf_op jit(solution)/shard_map/pack_rest/pallas_call | solution.py:100
  67.8 3.9 constant_dynamic-slice_fusion.1
  75.3 17.3 %collective-permute-done.57.refs_6_.refs_11_ = bf16[2,512,512]{2,1,0:T(8,128)(2,1)S(1)} collective-permute-done((bf16[2,512,512]{2,1,0:T(8,128)(2,1)S(1)}, bf16[2,512,512]{2,1,0:T(8,128)(2,1)S(1)}, u32[]{:S(2)}, u32[]{:S(2)}) %collective-permute-start.57) | collective-permute-done | bytes 1048608 | tf_op jit(solution)/shard_map/ppermute | solution.py:49
  101.4 5.5 dynamic-slice_bitcast_fusion.refs_8_.refs_13_
  107.4 9.0 build_send.1
  116.4 44.7 %collective-permute-done.58.refs_7_.refs_12_ = bf16[2,512,512]{2,1,0:T(8,128)(2,1)} collective-permute-done((bf16[2,512,512]{2,1,0:T(8,128)(2,1)}, bf16[2,512,512]{2,1,0:T(8,128)(2,1)}, u32[]{:S(2)}, u32[]{:S(2)}) %collective-permute-start.58) | collective-permute-done | bytes 1048608 | tf_op jit(solution)/shard_map/ppermute | solution.py:53
  164.6 39.0 %collective-permute-done.54 = bf16[2,768,2048]{2,1,0:T(8,128)(2,1)} collective-permute-done((bf16[2,768,2048]{2,1,0:T(8,128)(2,1)}, bf16[2,768,2048]{2,1,0:T(8,128)(2,1)}, u32[]{:S(2)}, u32[]{:S(2)}) %collective-permute-start.54) | collective-permute-done | bytes 6291488 | tf_op jit(solution)/shard_map/ppermute | solution.py:57
  205.3 49.7 %shard_map.69 = (f32[2,256,2048]{2,1,0:T(8,128)}, f32[2,256,2048]{2,1,0:T(8,128)}) custom-call(s32[64]{0:T(128)S(1)} %and_select_fusion.4.tab_ref, s32[4]{0:T(128)S(1)} %fusion.6.info_ref, bf16[2,768,2048]{2,1,0:T(8,128)(2,1)} %pad_maximum_fusion.refs_0_, bf16[2,768,2048]{2,1,0:T(8,128)(2,1)} %collective-permute-done.53.refs_1_, ...), custom_call_target="tpu_custom_call" | custom-call | flops 34359738368 | bytes 200000000 | tf_op jit(solution)/shard_map/pallas_call | solution.py:375
  255.1 49.5 %shard_map.68 = (f32[2,256,2048]{2,1,0:T(8,128)}, f32[2,256,2048]{2,1,0:T(8,128)}) custom-call(s32[64]{0:T(128)S(1)} %and_select_fusion.4.tab_ref, s32[4]{0:T(128)S(1)} %fusion.6.info_ref, bf16[2,768,2048]{2,1,0:T(8,128)(2,1)} %pad_maximum_fusion.refs_0_, bf16[2,768,2048]{2,1,0:T(8,128)(2,1)} %collective-permute-done.53.refs_1_, ...), custom_call_target="tpu_custom_call" | custom-call | flops 34359738368 | bytes 200000000 | tf_op jit(solution)/shard_map/pallas_call | solution.py:375
  304.6 395.7 %conditional.1 = (bf16[2,768,2048]{2,1,0:T(8,128)(2,1)}, bf16[2,768,2048]{2,1,0:T(8,128)(2,1)}, bf16[2,384,2048]{2,1,0:T(8,128)(2,1)}, bf16[2,768,2048]{2,1,0:T(...) conditional(s32[]{:T(128)} %clamp.3, (s32[64]{0:T(128)S(1)}, ...), branch_computations={%region_4.5_spmd, %region_5.6_spmd, %region_6.7_spmd, %region_7.8_... | conditional | flops 85899345920 | bytes 338412288 | solution.py:690
  319.3 22.4 %collective-permute-start.22 = (bf16[2,768,2048]{2,1,0:T(8,128)(2,1)}, bf16[2,768,2048]{2,1,0:T(8,128)(2,1)}, u32[]{:S(2)}, u32[]{:S(2)}) collective-permute-start(bf16[2,768,2048]{2,1,0:T(8,128)(2,1)} %get-tuple-element.984), channel_id=1, source_target_pairs={{0,4},{4,0},{1,5},{5,1},{2,6},{6,2},{3,7},{7,3}} | collective-permute-start | bytes 18874376 | tf_op jit(solution)/shard_map/cond/branch_10_fun/ppermute | solution.py:57
  343.8 156.9 %collective-permute-done.21 = bf16[2,128,2048]{2,1,0:T(8,128)(2,1)S(1)} collective-permute-done((bf16[2,128,2048]{2,1,0:T(8,128)(2,1)S(1)}, bf16[2,128,2048]{2,1,0:T(8,128)(2,1)S(1)}, u32[]{:S(2)}, u32[]{:S(2)}) %collective-permute-start.21) | collective-permute-done | bytes 1048608 | tf_op jit(solution)/shard_map/cond/branch_10_fun/ppermute | solution.py:57
  501.2 177.8 %branch_10_fun.1 = (f32[8,256,2048]{2,1,0:T(8,128)}, f32[8,256,2048]{2,1,0:T(8,128)}) custom-call(s32[64]{0:T(128)S(1)} %get-tuple-element.986.tab_ref, s32[4]{0:T(128)S(1)} %get-tuple-element.987.info_ref, bf16[2,768,2048]{2,1,0:T(8,128)(2,1)} %get-tuple-element.988.refs_0_, bf16[2,768,2048]{2,1,0:T(8,128)(2,1)} %get-tuple-element.989.refs_1_, ...), custom_call_target="tpu_custom_call" | custom-call | flops 85899345920 | bytes 200000000 | tf_op jit(solution)/shard_map/cond/branch_10_fun/pallas_call | solution.py:375
  679.0 3.4 pad.56
  682.4 3.4 pad.57
  703.1 3.1 collective-permute-done.64.refs_7_
  706.2 4.6 collective-permute-done.63.refs_4_
  710.8 25.3 %shard_map.71 = (f32[128,2048]{1,0:T(8,128)S(1)}, f32[256,1024]{1,0:T(8,128)S(1)}, f32[128,2048]{1,0:T(8,128)}, f32[128,2048]{1,0:T(8,128)S(1)}) custom-call(s32[40]{0:T(128)S(1)} %compare_select_fusion.6.tab_ref, s32[3]{0:T(128)S(1)} %pad_add_fusion.4.info_ref, bf16[2,384,2048]{2,1,0:T(8,128)(2,1)} %collective-permute-done.52.refs_0_, ...), custom_call_target="tpu_custom_call" | custom-call | flops 12884901888 | bytes 40000000 | tf_op jit(solution)/shard_map/pallas_call | solution.py:436
  738.2 25.0 %shard_map.70 = (f32[128,2048]{1,0:T(8,128)S(1)}, f32[256,1024]{1,0:T(8,128)S(1)}, f32[128,2048]{1,0:T(8,128)}, f32[128,2048]{1,0:T(8,128)S(1)}) custom-call(s32[40]{0:T(128)S(1)} %compare_select_fusion.6.tab_ref, s32[3]{0:T(128)S(1)} %pad_add_fusion.4.info_ref, bf16[2,384,2048]{2,1,0:T(8,128)(2,1)} %collective-permute-done.52.refs_0_, ...), custom_call_target="tpu_custom_call" | custom-call | flops 12884901888 | bytes 40000000 | tf_op jit(solution)/shard_map/pallas_call | solution.py:436
  767.2 15.1 %collective-permute-start.70 = (f32[2,512,128]{2,1,0:T(8,128)S(1)}, f32[2,512,128]{2,1,0:T(8,128)S(1)}, u32[]{:S(2)}, u32[]{:S(2)}) collective-permute-start(f32[2,512,128]{2,1,0:T(8,128)S(1)} %get-tuple-element.1286.refs_17_), channel_id=1, source_target_pairs={{0,4},{4,0},{1,5},{5,1},{2,6},{6,2},{3,7},{7,3}} | collective-permute-start | bytes 1572872 | tf_op jit(solution)/shard_map/ppermute | solution.py:57
  782.3 25.5 %shard_map.76 = (f32[128,2048]{1,0:T(8,128)S(1)}, f32[256,1024]{1,0:T(8,128)S(1)}, f32[128,2048]{1,0:T(8,128)}, f32[128,2048]{1,0:T(8,128)}) custom-call(s32[40]{0:T(128)S(1)} %compare_select_fusion.6.tab_ref, s32[3]{0:T(128)S(1)} %pad_add_fusion.4.info_ref, bf16[2,384,2048]{2,1,0:T(8,128)(2,1)} %collective-permute-done.52.refs_0_, ...), custom_call_target="tpu_custom_call" | custom-call | flops 12884901888 | bytes 40000000 | tf_op jit(solution)/shard_map/pallas_call | solution.py:436
  809.6 25.5 %shard_map.74 = (f32[128,2048]{1,0:T(8,128)S(1)}, f32[256,1024]{1,0:T(8,128)S(1)}, f32[128,2048]{1,0:T(8,128)}, f32[128,2048]{1,0:T(8,128)}) custom-call(s32[40]{0:T(128)S(1)} %compare_select_fusion.6.tab_ref, s32[3]{0:T(128)S(1)} %pad_add_fusion.4.info_ref, bf16[2,384,2048]{2,1,0:T(8,128)(2,1)} %collective-permute-done.52.refs_0_, ...), custom_call_target="tpu_custom_call" | custom-call | flops 12884901888 | bytes 40000000 | tf_op jit(solution)/shard_map/pallas_call | solution.py:436
  835.1 10.1 collective-permute-start.71
  855.2 19.0 %collective-permute-start.69 = (f32[128,2048]{1,0:T(8,128)}, f32[128,2048]{1,0:T(8,128)S(1)}, u32[]{:S(2)}, u32[]{:S(2)}) collective-permute-start(f32[128,2048]{1,0:T(8,128)} %get-tuple-element.1285), channel_id=1, source_target_pairs={{0,4},{4,0},{1,5},{5,1},{2,6},{6,2},{3,7},{7,3}} | collective-permute-start | bytes 3145736 | tf_op jit(solution)/shard_map/ppermute | solution.py:57
  874.1 25.5 %shard_map.83 = (f32[128,2048]{1,0:T(8,128)S(1)}, f32[256,1024]{1,0:T(8,128)S(1)}, f32[128,2048]{1,0:T(8,128)}, f32[128,2048]{1,0:T(8,128)}) custom-call(s32[40]{0:T(128)S(1)} %compare_select_fusion.6.tab_ref, s32[3]{0:T(128)S(1)} %pad_add_fusion.4.info_ref, bf16[2,384,2048]{2,1,0:T(8,128)(2,1)} %collective-permute-done.52.refs_0_, ...), custom_call_target="tpu_custom_call" | custom-call | flops 12884901888 | bytes 40000000 | tf_op jit(solution)/shard_map/pallas_call | solution.py:436
  899.7 18.6 %collective-permute-done.73.rc = f32[128,2048]{1,0:T(8,128)S(1)} collective-permute-done((f32[128,2048]{1,0:T(8,128)}, f32[128,2048]{1,0:T(8,128)S(1)}, u32[]{:S(2)}, u32[]{:S(2)}) %collective-permute-start.73) | collective-permute-done | bytes 1048608 | tf_op jit(solution)/shard_map/ppermute | solution.py:49
  919.0 18.0 %collective-permute-start.84 = (f32[2,512,128]{2,1,0:T(8,128)}, f32[2,512,128]{2,1,0:T(8,128)S(1)}, u32[]{:S(2)}, u32[]{:S(2)}) collective-permute-start(f32[2,512,128]{2,1,0:T(8,128)} %copy-done.17), channel_id=1, source_target_pairs={{0,5},{1,4},{2,7},{3,6},{4,1},{5,0},{6,3},{7,2}} | collective-permute-start | bytes 1572872 | tf_op jit(solution)/shard_map/ppermute | solution.py:61
  946.2 3.4 collective-permute-done.84.uy_ref
  951.7 24.7 %shard_map.82 = (f32[128,2048]{1,0:T(8,128)S(1)}, f32[256,1024]{1,0:T(8,128)S(1)}, f32[128,2048]{1,0:T(8,128)S(1)}, f32[128,2048]{1,0:T(8,128)S(1)}) custom-call(s32[40]{0:T(128)S(1)} %compare_select_fusion.6.tab_ref, s32[3]{0:T(128)S(1)} %pad_add_fusion.4.info_ref, bf16[2,384,2048]{2,1,0:T(8,128)(2,1)} %collective-permute-done.52.refs_0_, ...), custom_call_target="tpu_custom_call" | custom-call | flops 12884901888 | bytes 40000000 | tf_op jit(solution)/shard_map/pallas_call | solution.py:436
  978.3 5.2 collective-permute-done.78.uc_ref
  992.3 24.7 %collective-permute-done.79.uy_ref = f32[2,512,128]{2,1,0:T(8,128)S(1)} collective-permute-done((f32[2,512,128]{2,1,0:T(8,128)}, f32[2,512,128]{2,1,0:T(8,128)S(1)}, u32[]{:S(2)}, u32[]{:S(2)}) %collective-permute-start.79) | collective-permute-done | bytes 524320 | tf_op jit(solution)/shard_map/ppermute | solution.py:61
  1025.6 2.9 collective-permute-done.95.uc_ref
  1030.6 8.7 collective-permute-done.96.uy_ref
  1040.5 25.6 %shard_map.91 = (f32[128,2048]{1,0:T(8,128)S(1)}, f32[256,1024]{1,0:T(8,128)S(1)}, f32[128,2048]{1,0:T(8,128)}, f32[128,2048]{1,0:T(8,128)}) custom-call(s32[40]{0:T(128)S(1)} %compare_select_fusion.6.tab_ref, s32[3]{0:T(128)S(1)} %pad_add_fusion.4.info_ref, bf16[2,384,2048]{2,1,0:T(8,128)(2,1)} %collective-permute-done.52.refs_0_, ...), custom_call_target="tpu_custom_call" | custom-call | flops 12884901888 | bytes 40000000 | tf_op jit(solution)/shard_map/pallas_call | solution.py:436
  1067.3 6.1 collective-permute-done.110.uc_ref
  1075.8 8.8 collective-permute-done.90.uc_ref
  1086.8 24.4 %shard_map.90 = (f32[128,2048]{1,0:T(8,128)S(1)}, f32[256,1024]{1,0:T(8,128)S(1)}, f32[128,2048]{1,0:T(8,128)S(1)}, f32[128,2048]{1,0:T(8,128)S(1)}) custom-call(s32[40]{0:T(128)S(1)} %compare_select_fusion.6.tab_ref, s32[3]{0:T(128)S(1)} %pad_add_fusion.4.info_ref, bf16[2,384,2048]{2,1,0:T(8,128)(2,1)} %collective-permute-done.52.refs_0_, ...), custom_call_target="tpu_custom_call" | custom-call | flops 12884901888 | bytes 40000000 | tf_op jit(solution)/shard_map/pallas_call | solution.py:436
  1118.3 6.0 collective-permute-done.99.rc
  1127.8 3.3 shard_map.96
  1131.2 20.6 %collective-permute-done.111.uy_ref = f32[2,512,128]{2,1,0:T(8,128)S(1)} collective-permute-done((f32[2,512,128]{2,1,0:T(8,128)S(1)}, f32[2,512,128]{2,1,0:T(8,128)S(1)}, u32[]{:S(2)}, u32[]{:S(2)}) %collective-permute-start.111) | collective-permute-done | bytes 524320 | tf_op jit(solution)/shard_map/ppermute | solution.py:61
  1153.9 12.8 %collective-permute-done.101.rc = f32[128,2048]{1,0:T(8,128)S(1)} collective-permute-done((f32[128,2048]{1,0:T(8,128)S(1)}, f32[128,2048]{1,0:T(8,128)S(1)}, u32[]{:S(2)}, u32[]{:S(2)}) %collective-permute-start.101) | collective-permute-done | bytes 1048608 | tf_op jit(solution)/shard_map/ppermute | solution.py:49
  1172.3 25.9 %collective-permute-done.106.uc_ref = f32[2,512,128]{2,1,0:T(8,128)S(1)} collective-permute-done((f32[2,512,128]{2,1,0:T(8,128)S(1)}, f32[2,512,128]{2,1,0:T(8,128)S(1)}, u32[]{:S(2)}, u32[]{:S(2)}) %collective-permute-start.106) | collective-permute-done | bytes 524320 | tf_op jit(solution)/shard_map/ppermute | solution.py:57
  1204.9 36.8 %collective-permute-done.102.uc_ref = f32[2,512,128]{2,1,0:T(8,128)S(1)} collective-permute-done((f32[2,512,128]{2,1,0:T(8,128)S(1)}, f32[2,512,128]{2,1,0:T(8,128)S(1)}, u32[]{:S(2)}, u32[]{:S(2)}) %collective-permute-start.102) | collective-permute-done | bytes 524320 | tf_op jit(solution)/shard_map/ppermute | solution.py:57
  (217 shorter events, 113.0 us)
Async XLA Ops:
  64.7 42.2 %collective-permute-start.51 = (bf16[2,2432,2048]{2,1,0:T(8,128)(2,1)}, bf16[2,2432,2048]{2,1,0:T(8,128)(2,1)}, u32[]{:S(2)}, u32[]{:S(2)}) collective-permute-start(bf16[2,2432,2048]{2,1,0:T(8,128)(2,1)} %pack_rest.1.own_ref.refs_2_.refs_8_), channel_id=1, source_target_pairs={{0,1},{1,0},{2,3},{3,2},{4,5},{5,4},{6,7},{7,6}} | collective-permute-start | bytes 59768840 | tf_op jit(solution)/shard_map/ppermute | solution.py:45
  64.7 138.8 %collective-permute-start.54 = (bf16[2,768,2048]{2,1,0:T(8,128)(2,1)}, bf16[2,768,2048]{2,1,0:T(8,128)(2,1)}, u32[]{:S(2)}, u32[]{:S(2)}) collective-permute-start(bf16[2,768,2048]{2,1,0:T(8,128)(2,1)} %pad_maximum_fusion.refs_0_), channel_id=1, source_target_pairs={{0,4},{4,0},{1,5},{5,1},{2,6},{6,2},{3,7},{7,3}} | collective-permute-start | bytes 18874376 | tf_op jit(solution)/shard_map/ppermute | solution.py:57
  67.1 136.5 %collective-permute-start.53 = (bf16[2,768,2048]{2,1,0:T(8,128)(2,1)}, bf16[2,768,2048]{2,1,0:T(8,128)(2,1)}, u32[]{:S(2)}, u32[]{:S(2)}) collective-permute-start(bf16[2,768,2048]{2,1,0:T(8,128)(2,1)} %pad_maximum_fusion.refs_0_), channel_id=1, source_target_pairs={{0,1},{1,0},{2,3},{3,2},{4,5},{5,4},{6,7},{7,6}} | collective-permute-start | bytes 18874376 | tf_op jit(solution)/shard_map/ppermute | solution.py:45
  73.3 88.8 %collective-permute-start.56 = (bf16[2,512,1024]{2,1,0:T(8,128)(2,1)}, bf16[2,512,1024]{2,1,0:T(8,128)(2,1)}, u32[]{:S(2)}, u32[]{:S(2)}) collective-permute-start(bf16[2,512,1024]{2,1,0:T(8,128)(2,1)} %pad_maximum_fusion.2), channel_id=1, source_target_pairs={{0,1},{1,0},{2,3},{3,2},{4,5},{5,4},{6,7},{7,6}} | collective-permute-start | bytes 6291464 | tf_op jit(solution)/shard_map/ppermute | solution.py:45
  92.7 71.4 %collective-permute-start.59 = (bf16[512,2048]{1,0:T(8,128)(2,1)}, bf16[512,2048]{1,0:T(8,128)(2,1)}, u32[]{:S(2)}, u32[]{:S(2)}) collective-permute-start(bf16[512,2048]{1,0:T(8,128)(2,1)} %get-tuple-element.1257), channel_id=1, source_target_pairs={{0,2},{2,0},{1,3},{3,1},{4,6},{6,4},{5,7},{7,5}} | collective-permute-start | bytes 6291464 | tf_op jit(solution)/shard_map/ppermute | solution.py:49
  106.9 54.2 %collective-permute-start.58 = (bf16[2,512,512]{2,1,0:T(8,128)(2,1)}, bf16[2,512,512]{2,1,0:T(8,128)(2,1)}, u32[]{:S(2)}, u32[]{:S(2)}) collective-permute-start(bf16[2,512,512]{2,1,0:T(8,128)(2,1)} %get-tuple-element.1256), channel_id=1, source_target_pairs={{0,3},{3,0},{1,2},{2,1},{4,7},{7,4},{5,6},{6,5}} | collective-permute-start | bytes 3145736 | tf_op jit(solution)/shard_map/ppermute | solution.py:53
  161.1 143.4 %collective-permute-start.60 = (bf16[2,512,512]{2,1,0:T(8,128)(2,1)}, bf16[2,512,512]{2,1,0:T(8,128)(2,1)}, u32[]{:S(2)}, u32[]{:S(2)}) collective-permute-start(bf16[2,512,512]{2,1,0:T(8,128)(2,1)} %get-tuple-element.1258), channel_id=1, source_target_pairs={{0,2},{2,0},{1,3},{3,1},{4,6},{6,4},{5,7},{7,5}} | collective-permute-start | bytes 3145736 | tf_op jit(solution)/shard_map/ppermute | solution.py:49
  162.1 142.4 %collective-permute-start.61 = (bf16[2,512,512]{2,1,0:T(8,128)(2,1)}, bf16[2,512,512]{2,1,0:T(8,128)(2,1)}, u32[]{:S(2)}, u32[]{:S(2)}) collective-permute-start(bf16[2,512,512]{2,1,0:T(8,128)(2,1)} %get-tuple-element.1259), channel_id=1, source_target_pairs={{0,3},{3,0},{1,2},{2,1},{4,7},{7,4},{5,6},{6,5}} | collective-permute-start | bytes 3145736 | tf_op jit(solution)/shard_map/ppermute | solution.py:53
  164.0 140.5 %collective-permute-start.62 = (bf16[512,2048]{1,0:T(8,128)(2,1)}, bf16[512,2048]{1,0:T(8,128)(2,1)}, u32[]{:S(2)}, u32[]{:S(2)}) collective-permute-start(bf16[512,2048]{1,0:T(8,128)(2,1)} %get-tuple-element.1260), channel_id=1, source_target_pairs={{0,2},{2,0},{1,3},{3,1},{4,6},{6,4},{5,7},{7,5}} | collective-permute-start | bytes 6291464 | tf_op jit(solution)/shard_map/ppermute | solution.py:49
  203.6 101.0 %collective-permute-start.55 = (bf16[2,768,2048]{2,1,0:T(8,128)(2,1)}, bf16[2,768,2048]{2,1,0:T(8,128)(2,1)}, u32[]{:S(2)}, u32[]{:S(2)}) collective-permute-start(bf16[2,768,2048]{2,1,0:T(8,128)(2,1)} %collective-permute-done.54), channel_id=1, source_target_pairs={{0,1},{1,0},{2,3},{3,2},{4,5},{5,4},{6,7},{7,6}} | collective-permute-start | bytes 18874376 | tf_op jit(solution)/shard_map/ppermute | solution.py:45
  203.6 496.8 %collective-permute-start.52 = (bf16[2,384,2048]{2,1,0:T(8,128)(2,1)}, bf16[2,384,2048]{2,1,0:T(8,128)(2,1)}, u32[]{:S(2)}, u32[]{:S(2)}) collective-permute-start(bf16[2,384,2048]{2,1,0:T(8,128)(2,1)} %get-tuple-element.1253), channel_id=1, source_target_pairs={{0,4},{4,0},{1,5},{5,1},{2,6},{6,2},{3,7},{7,3}} | collective-permute-start | bytes 9437192 | tf_op jit(solution)/shard_map/ppermute | solution.py:57
  319.3 181.5 %collective-permute-start.22 = (bf16[2,768,2048]{2,1,0:T(8,128)(2,1)}, bf16[2,768,2048]{2,1,0:T(8,128)(2,1)}, u32[]{:S(2)}, u32[]{:S(2)}) collective-permute-start(bf16[2,768,2048]{2,1,0:T(8,128)(2,1)} %get-tuple-element.984), channel_id=1, source_target_pairs={{0,4},{4,0},{1,5},{5,1},{2,6},{6,2},{3,7},{7,3}} | collective-permute-start | bytes 18874376 | tf_op jit(solution)/shard_map/cond/branch_10_fun/ppermute | solution.py:57
  341.8 158.9 %collective-permute-start.21 = (bf16[2,128,2048]{2,1,0:T(8,128)(2,1)S(1)}, bf16[2,128,2048]{2,1,0:T(8,128)(2,1)S(1)}, u32[]{:S(2)}, u32[]{:S(2)}) collective-permute-start(bf16[2,128,2048]{2,1,0:T(8,128)(2,1)S(1)} %slice.47), channel_id=1, source_target_pairs={{0,4},{4,0},{1,5},{5,1},{2,6},{6,2},{3,7},{7,3}} | collective-permute-start | bytes 3145736 | tf_op jit(solution)/shard_map/cond/branch_10_fun/ppermute | solution.py:57
  341.8 344.0 %collective-permute-start.23 = (bf16[2,384,2048]{2,1,0:T(8,128)(2,1)}, bf16[2,384,2048]{2,1,0:T(8,128)(2,1)}, u32[]{:S(2)}, u32[]{:S(2)}) collective-permute-start(bf16[2,384,2048]{2,1,0:T(8,128)(2,1)} %get-tuple-element.985), channel_id=1, source_target_pairs={{0,4},{4,0},{1,5},{5,1},{2,6},{6,2},{3,7},{7,3}} | collective-permute-start | bytes 9437192 | tf_op jit(solution)/shard_map/cond/branch_10_fun/ppermute | solution.py:57
  500.7 181.7 %collective-permute-start.24 = (bf16[2,128,2048]{2,1,0:T(8,128)(2,1)S(1)}, bf16[2,128,2048]{2,1,0:T(8,128)(2,1)S(1)}, u32[]{:S(2)}, u32[]{:S(2)}) collective-permute-start(bf16[2,128,2048]{2,1,0:T(8,128)(2,1)S(1)} %collective-permute-done.21), channel_id=1, source_target_pairs={{0,1},{1,0},{2,3},{3,2},{4,5},{5,4},{6,7},{7,6}} | collective-permute-start | bytes 3145736 | tf_op jit(solution)/shard_map/cond/branch_10_fun/ppermute | solution.py:45
  500.7 185.1 %collective-permute-start.25 = (bf16[2,768,2048]{2,1,0:T(8,128)(2,1)}, bf16[2,768,2048]{2,1,0:T(8,128)(2,1)}, u32[]{:S(2)}, u32[]{:S(2)}) collective-permute-start(bf16[2,768,2048]{2,1,0:T(8,128)(2,1)} %collective-permute-done.22), channel_id=1, source_target_pairs={{0,1},{1,0},{2,3},{3,2},{4,5},{5,4},{6,7},{7,6}} | collective-permute-start | bytes 18874376 | tf_op jit(solution)/shard_map/cond/branch_10_fun/ppermute | solution.py:45
  736.2 98.9 %collective-permute-start.68 = (f32[128,2048]{1,0:T(8,128)}, f32[128,2048]{1,0:T(8,128)}, u32[]{:S(2)}, u32[]{:S(2)}) collective-permute-start(f32[128,2048]{1,0:T(8,128)} %get-tuple-element.1284), channel_id=1, source_target_pairs={{0,2},{2,0},{1,3},{3,1},{4,6},{6,4},{5,7},{7,5}} | collective-permute-start | bytes 3145736 | tf_op jit(solution)/shard_map/ppermute | solution.py:49
  763.2 44.5 %collective-permute-start.65 = (f32[128,2048]{1,0:T(8,128)S(1)}, f32[128,2048]{1,0:T(8,128)S(1)}, u32[]{:S(2)}, u32[]{:S(2)}) collective-permute-start(f32[128,2048]{1,0:T(8,128)S(1)} %get-tuple-element.1276), channel_id=1, source_target_pairs={{0,2},{2,0},{1,3},{3,1},{4,6},{6,4},{5,7},{7,5}} | collective-permute-start | bytes 3145736 | tf_op jit(solution)/shard_map/ppermute | solution.py:49
  763.3 84.6 %collective-permute-start.74 = (f32[128,2048]{1,0:T(8,128)}, f32[128,2048]{1,0:T(8,128)S(1)}, u32[]{:S(2)}, u32[]{:S(2)}) collective-permute-start(f32[128,2048]{1,0:T(8,128)} %get-tuple-element.1291), channel_id=1, source_target_pairs={{0,2},{2,0},{1,3},{3,1},{4,6},{6,4},{5,7},{7,5}} | collective-permute-start | bytes 3145736 | tf_op jit(solution)/shard_map/ppermute | solution.py:49
  767.2 86.6 %collective-permute-start.70 = (f32[2,512,128]{2,1,0:T(8,128)S(1)}, f32[2,512,128]{2,1,0:T(8,128)S(1)}, u32[]{:S(2)}, u32[]{:S(2)}) collective-permute-start(f32[2,512,128]{2,1,0:T(8,128)S(1)} %get-tuple-element.1286.refs_17_), channel_id=1, source_target_pairs={{0,4},{4,0},{1,5},{5,1},{2,6},{6,2},{3,7},{7,3}} | collective-permute-start | bytes 1572872 | tf_op jit(solution)/shard_map/ppermute | solution.py:57
  782.3 72.9 %collective-permute-start.72 = (f32[2,512,128]{2,1,0:T(8,128)}, f32[2,512,128]{2,1,0:T(8,128)S(1)}, u32[]{:S(2)}, u32[]{:S(2)}) collective-permute-start(f32[2,512,128]{2,1,0:T(8,128)} %get-tuple-element.1287), channel_id=1, source_target_pairs={{0,1},{1,0},{2,3},{3,2},{4,5},{5,4},{6,7},{7,6}} | collective-permute-start | bytes 1572872 | tf_op jit(solution)/shard_map/ppermute | solution.py:45
  807.8 43.5 %collective-permute-start.75 = (f32[128,2048]{1,0:T(8,128)}, f32[128,2048]{1,0:T(8,128)S(1)}, u32[]{:S(2)}, u32[]{:S(2)}) collective-permute-start(f32[128,2048]{1,0:T(8,128)} %get-tuple-element.1296), channel_id=1, source_target_pairs={{0,2},{2,0},{1,3},{3,1},{4,6},{6,4},{5,7},{7,5}} | collective-permute-start | bytes 3145736 | tf_op jit(solution)/shard_map/ppermute | solution.py:49
  835.1 64.5 %collective-permute-start.71 = (f32[2,512,128]{2,1,0:T(8,128)}, f32[2,512,128]{2,1,0:T(8,128)S(1)}, u32[]{:S(2)}, u32[]{:S(2)}) collective-permute-start(f32[2,512,128]{2,1,0:T(8,128)} %get-tuple-element.1287), channel_id=1, source_target_pairs={{0,5},{1,4},{2,7},{3,6},{4,1},{5,0},{6,3},{7,2}} | collective-permute-start | bytes 1572872 | tf_op jit(solution)/shard_map/ppermute | solution.py:61
  847.9 93.3 %collective-permute-start.67 = (f32[128,2048]{1,0:T(8,128)}, f32[128,2048]{1,0:T(8,128)S(1)}, u32[]{:S(2)}, u32[]{:S(2)}) collective-permute-start(f32[128,2048]{1,0:T(8,128)} %get-tuple-element.1282), channel_id=1, source_target_pairs={{0,2},{2,0},{1,3},{3,1},{4,6},{6,4},{5,7},{7,5}} | collective-permute-start | bytes 3145736 | tf_op jit(solution)/shard_map/ppermute | solution.py:49
  851.3 99.4 %collective-permute-start.86 = (f32[128,2048]{1,0:T(8,128)}, f32[128,2048]{1,0:T(8,128)S(1)}, u32[]{:S(2)}, u32[]{:S(2)}) collective-permute-start(f32[128,2048]{1,0:T(8,128)} %get-tuple-element.1311), channel_id=1, source_target_pairs={{0,2},{2,0},{1,3},{3,1},{4,6},{6,4},{5,7},{7,5}} | collective-permute-start | bytes 3145736 | tf_op jit(solution)/shard_map/ppermute | solution.py:49
  853.8 64.5 %collective-permute-start.73 = (f32[128,2048]{1,0:T(8,128)}, f32[128,2048]{1,0:T(8,128)S(1)}, u32[]{:S(2)}, u32[]{:S(2)}) collective-permute-start(f32[128,2048]{1,0:T(8,128)} %get-tuple-element.1289), channel_id=1, source_target_pairs={{0,2},{2,0},{1,3},{3,1},{4,6},{6,4},{5,7},{7,5}} | collective-permute-start | bytes 3145736 | tf_op jit(solution)/shard_map/ppermute | solution.py:49
  855.2 63.8 %collective-permute-start.69 = (f32[128,2048]{1,0:T(8,128)}, f32[128,2048]{1,0:T(8,128)S(1)}, u32[]{:S(2)}, u32[]{:S(2)}) collective-permute-start(f32[128,2048]{1,0:T(8,128)} %get-tuple-element.1285), channel_id=1, source_target_pairs={{0,4},{4,0},{1,5},{5,1},{2,6},{6,2},{3,7},{7,3}} | collective-permute-start | bytes 3145736 | tf_op jit(solution)/shard_map/ppermute | solution.py:57
  899.6 44.3 %collective-permute-start.83 = (f32[2,512,128]{2,1,0:T(8,128)S(1)}, f32[2,512,128]{2,1,0:T(8,128)S(1)}, u32[]{:S(2)}, u32[]{:S(2)}) collective-permute-start(f32[2,512,128]{2,1,0:T(8,128)S(1)} %get-tuple-element.1280.refs_17_), channel_id=1, source_target_pairs={{0,4},{4,0},{1,5},{5,1},{2,6},{6,2},{3,7},{7,3}} | collective-permute-start | bytes 1572872 | tf_op jit(solution)/shard_map/ppermute | solution.py:57
  950.4 66.7 %collective-permute-start.87 = (f32[128,2048]{1,0:T(8,128)}, f32[128,2048]{1,0:T(8,128)S(1)}, u32[]{:S(2)}, u32[]{:S(2)}) collective-permute-start(f32[128,2048]{1,0:T(8,128)} %get-tuple-element.1318), channel_id=1, source_target_pairs={{0,2},{2,0},{1,3},{3,1},{4,6},{6,4},{5,7},{7,5}} | collective-permute-start | bytes 3145736 | tf_op jit(solution)/shard_map/ppermute | solution.py:49
  950.7 70.0 %collective-permute-start.77 = (f32[128,2048]{1,0:T(8,128)}, f32[128,2048]{1,0:T(8,128)S(1)}, u32[]{:S(2)}, u32[]{:S(2)}) collective-permute-start(f32[128,2048]{1,0:T(8,128)} %get-tuple-element.1303), channel_id=1, source_target_pairs={{0,4},{4,0},{1,5},{5,1},{2,6},{6,2},{3,7},{7,3}} | collective-permute-start | bytes 3145736 | tf_op jit(solution)/shard_map/ppermute | solution.py:57
  1020.7 45.3 %collective-permute-start.98 = (f32[128,2048]{1,0:T(8,128)S(1)}, f32[128,2048]{1,0:T(8,128)S(1)}, u32[]{:S(2)}, u32[]{:S(2)}) collective-permute-start(f32[128,2048]{1,0:T(8,128)S(1)} %copy-done.10), channel_id=1, source_target_pairs={{0,2},{2,0},{1,3},{3,1},{4,6},{6,4},{5,7},{7,5}} | collective-permute-start | bytes 3145736 | tf_op jit(solution)/shard_map/ppermute | solution.py:49
  1023.3 44.0 %collective-permute-start.94 = (f32[128,2048]{1,0:T(8,128)}, f32[128,2048]{1,0:T(8,128)S(1)}, u32[]{:S(2)}, u32[]{:S(2)}) collective-permute-start(f32[128,2048]{1,0:T(8,128)} %get-tuple-element.1330), channel_id=1, source_target_pairs={{0,4},{4,0},{1,5},{5,1},{2,6},{6,2},{3,7},{7,3}} | collective-permute-start | bytes 3145736 | tf_op jit(solution)/shard_map/ppermute | solution.py:57
  1028.5 44.9 %collective-permute-start.110 = (f32[2,512,128]{2,1,0:T(8,128)S(1)}, f32[2,512,128]{2,1,0:T(8,128)S(1)}, u32[]{:S(2)}, u32[]{:S(2)}) collective-permute-start(f32[2,512,128]{2,1,0:T(8,128)S(1)} %get-tuple-element.1322.refs_17_), channel_id=1, source_target_pairs={{0,4},{4,0},{1,5},{5,1},{2,6},{6,2},{3,7},{7,3}} | collective-permute-start | bytes 1572872 | tf_op jit(solution)/shard_map/ppermute | solution.py:57
  1030.6 44.9 %collective-permute-start.112 = (f32[2,512,128]{2,1,0:T(8,128)S(1)}, f32[2,512,128]{2,1,0:T(8,128)S(1)}, u32[]{:S(2)}, u32[]{:S(2)}) collective-permute-start(f32[2,512,128]{2,1,0:T(8,128)S(1)} %get-tuple-element.1354), channel_id=1, source_target_pairs={{0,1},{1,0},{2,3},{3,2},{4,5},{5,4},{6,7},{7,6}} | collective-permute-start | bytes 1572872 | tf_op jit(solution)/shard_map/ppermute | solution.py:45
  1039.4 45.3 %collective-permute-start.90 = (f32[2,512,128]{2,1,0:T(8,128)S(1)}, f32[2,512,128]{2,1,0:T(8,128)S(1)}, u32[]{:S(2)}, u32[]{:S(2)}) collective-permute-start(f32[2,512,128]{2,1,0:T(8,128)S(1)} %get-tuple-element.1326.refs_17_), channel_id=1, source_target_pairs={{0,4},{4,0},{1,5},{5,1},{2,6},{6,2},{3,7},{7,3}} | collective-permute-start | bytes 1572872 | tf_op jit(solution)/shard_map/ppermute | solution.py:57
  1066.1 46.1 %collective-permute-start.92 = (f32[2,512,128]{2,1,0:T(8,128)}, f32[2,512,128]{2,1,0:T(8,128)}, u32[]{:S(2)}, u32[]{:S(2)}) collective-permute-start(f32[2,512,128]{2,1,0:T(8,128)} %get-tuple-element.1327), channel_id=1, source_target_pairs={{0,1},{1,0},{2,3},{3,2},{4,5},{5,4},{6,7},{7,6}} | collective-permute-start | bytes 1572872 | tf_op jit(solution)/shard_map/ppermute | solution.py:45
  1067.3 44.8 %collective-permute-start.91 = (f32[2,512,128]{2,1,0:T(8,128)}, f32[2,512,128]{2,1,0:T(8,128)}, u32[]{:S(2)}, u32[]{:S(2)}) collective-permute-start(f32[2,512,128]{2,1,0:T(8,128)} %get-tuple-element.1327), channel_id=1, source_target_pairs={{0,5},{1,4},{2,7},{3,6},{4,1},{5,0},{6,3},{7,2}} | collective-permute-start | bytes 1572872 | tf_op jit(solution)/shard_map/ppermute | solution.py:61
  1073.4 54.4 %collective-permute-start.89 = (f32[128,2048]{1,0:T(8,128)}, f32[128,2048]{1,0:T(8,128)S(1)}, u32[]{:S(2)}, u32[]{:S(2)}) collective-permute-start(f32[128,2048]{1,0:T(8,128)} %get-tuple-element.1325), channel_id=1, source_target_pairs={{0,4},{4,0},{1,5},{5,1},{2,6},{6,2},{3,7},{7,3}} | collective-permute-start | bytes 3145736 | tf_op jit(solution)/shard_map/ppermute | solution.py:57
  1112.2 41.2 %collective-permute-start.88 = (f32[128,2048]{1,0:T(8,128)}, f32[128,2048]{1,0:T(8,128)S(1)}, u32[]{:S(2)}, u32[]{:S(2)}) collective-permute-start(f32[128,2048]{1,0:T(8,128)} %copy-done.11), channel_id=1, source_target_pairs={{0,2},{2,0},{1,3},{3,1},{4,6},{6,4},{5,7},{7,5}} | collective-permute-start | bytes 3145736 | tf_op jit(solution)/shard_map/ppermute | solution.py:49
  1112.2 54.5 %collective-permute-start.101 = (f32[128,2048]{1,0:T(8,128)S(1)}, f32[128,2048]{1,0:T(8,128)S(1)}, u32[]{:S(2)}, u32[]{:S(2)}) collective-permute-start(f32[128,2048]{1,0:T(8,128)S(1)} %get-tuple-element.1346), channel_id=1, source_target_pairs={{0,2},{2,0},{1,3},{3,1},{4,6},{6,4},{5,7},{7,5}} | collective-permute-start | bytes 3145736 | tf_op jit(solution)/shard_map/ppermute | solution.py:49
  1115.9 53.4 %collective-permute-start.109 = (f32[128,2048]{1,0:T(8,128)S(1)}, f32[128,2048]{1,0:T(8,128)S(1)}, u32[]{:S(2)}, u32[]{:S(2)}) collective-permute-start(f32[128,2048]{1,0:T(8,128)S(1)} %get-tuple-element.1353), channel_id=1, source_target_pairs={{0,4},{4,0},{1,5},{5,1},{2,6},{6,2},{3,7},{7,3}} | collective-permute-start | bytes 3145736 | tf_op jit(solution)/shard_map/ppermute | solution.py:57
  1127.8 74.8 %collective-permute-start.105 = (f32[128,2048]{1,0:T(8,128)S(1)}, f32[128,2048]{1,0:T(8,128)S(1)}, u32[]{:S(2)}, u32[]{:S(2)}) collective-permute-start(f32[128,2048]{1,0:T(8,128)S(1)} %get-tuple-element.1350), channel_id=1, source_target_pairs={{0,4},{4,0},{1,5},{5,1},{2,6},{6,2},{3,7},{7,3}} | collective-permute-start | bytes 3145736 | tf_op jit(solution)/shard_map/ppermute | solution.py:57
  1151.7 46.4 %collective-permute-start.108 = (f32[2,512,128]{2,1,0:T(8,128)S(1)}, f32[2,512,128]{2,1,0:T(8,128)S(1)}, u32[]{:S(2)}, u32[]{:S(2)}) collective-permute-start(f32[2,512,128]{2,1,0:T(8,128)S(1)} %get-tuple-element.1352), channel_id=1, source_target_pairs={{0,1},{1,0},{2,3},{3,2},{4,5},{5,4},{6,7},{7,6}} | collective-permute-start | bytes 1572872 | tf_op jit(solution)/shard_map/ppermute | solution.py:45
  1153.3 45.9 %collective-permute-start.107 = (f32[2,512,128]{2,1,0:T(8,128)S(1)}, f32[2,512,128]{2,1,0:T(8,128)S(1)}, u32[]{:S(2)}, u32[]{:S(2)}) collective-permute-start(f32[2,512,128]{2,1,0:T(8,128)S(1)} %get-tuple-element.1352), channel_id=1, source_target_pairs={{0,5},{1,4},{2,7},{3,6},{4,1},{5,0},{6,3},{7,2}} | collective-permute-start | bytes 1572872 | tf_op jit(solution)/shard_map/ppermute | solution.py:61
  1169.3 72.4 %collective-permute-start.100 = (f32[128,2048]{1,0:T(8,128)S(1)}, f32[128,2048]{1,0:T(8,128)S(1)}, u32[]{:S(2)}, u32[]{:S(2)}) collective-permute-start(f32[128,2048]{1,0:T(8,128)S(1)} %get-tuple-element.1344), channel_id=1, source_target_pairs={{0,4},{4,0},{1,5},{5,1},{2,6},{6,2},{3,7},{7,3}} | collective-permute-start | bytes 3145736 | tf_op jit(solution)/shard_map/ppermute | solution.py:57
  1198.2 43.6 %collective-permute-start.104 = (f32[2,512,128]{2,1,0:T(8,128)S(1)}, f32[2,512,128]{2,1,0:T(8,128)S(1)}, u32[]{:S(2)}, u32[]{:S(2)}) collective-permute-start(f32[2,512,128]{2,1,0:T(8,128)S(1)} %get-tuple-element.1349), channel_id=1, source_target_pairs={{0,1},{1,0},{2,3},{3,2},{4,5},{5,4},{6,7},{7,6}} | collective-permute-start | bytes 1572872 | tf_op jit(solution)/shard_map/ppermute | solution.py:45
  1198.2 43.6 %collective-permute-start.103 = (f32[2,512,128]{2,1,0:T(8,128)S(1)}, f32[2,512,128]{2,1,0:T(8,128)S(1)}, u32[]{:S(2)}, u32[]{:S(2)}) collective-permute-start(f32[2,512,128]{2,1,0:T(8,128)S(1)} %get-tuple-element.1349), channel_id=1, source_target_pairs={{0,5},{1,4},{2,7},{3,6},{4,1},{5,0},{6,3},{7,2}} | collective-permute-start | bytes 1572872 | tf_op jit(solution)/shard_map/ppermute | solution.py:61
  1199.3 42.5 %collective-permute-start.102 = (f32[2,512,128]{2,1,0:T(8,128)S(1)}, f32[2,512,128]{2,1,0:T(8,128)S(1)}, u32[]{:S(2)}, u32[]{:S(2)}) collective-permute-start(f32[2,512,128]{2,1,0:T(8,128)S(1)} %get-tuple-element.1348), channel_id=1, source_target_pairs={{0,4},{4,0},{1,5},{5,1},{2,6},{6,2},{3,7},{7,3}} | collective-permute-start | bytes 1572872 | tf_op jit(solution)/shard_map/ppermute | solution.py:57
  (46 other events, 1467.5 us)
